TPU v7x, 32 devices: a 4x2x2 block of a 4x4x8 slice. The times are simulated.
32 devices in a mesh: dp: 4 (over y, z), sp: 8 (over x, core).
Axes of the slice: x: 4, y: 2, z: 2, core: 2. Of those that a mesh axis runs over, the one named last changes fastest.
The devices are a block of a 4x4x8 slice.
Arguments:
- hidden: bfloat16 [512, 4096], P('dp'), parts along dimension 0
- w_norm: bfloat16 [4096], replicated
- w_q: bfloat16 [4096, 4096], replicated
- w_k: bfloat16 [4096, 256], replicated
- w_v: bfloat16 [4096, 256], replicated
- w_o: bfloat16 [4096, 4096], replicated
- k_cache: bfloat16 [512, 1024, 256], P('dp', 'sp'), parts along dimension 0
- v_cache: bfloat16 [512, 1024, 256], P('dp', 'sp'), parts along dimension 0
- cache_len: int32 [512], P('dp'), parts along dimension 0
Outputs:
- output 1: bfloat16 [512, 4096], P('dp'), parts along dimension 0
- output 2: bfloat16 [512, 1024, 256], P('dp', 'sp'), parts along dimension 0
- output 3: bfloat16 [512, 1024, 256], P('dp', 'sp'), parts along dimension 0
There are 4 independent parts. A program takes and returns all parts, laid end to end along the dimension named above; an argument that names none is the same for every part.
All inputs are finite; a program needn't handle non-finite values.
Results may differ from a plain program's by a relative error of at most 0.0135738.
Values sent between devices are 32-bit elements.
A program may use at most 768 MiB of HBM per device.

v0:
```python
import jax
import jax.numpy as jnp
from jax import lax
from jax.sharding import PartitionSpec as P

ROPE_BASE = 10000.0
EPSILON = 1e-6


def rotate_half(vectors, cos_t, sin_t):
    half_dim = vectors.shape[-1] // 2
    lower_half = vectors[..., :half_dim]
    upper_half = vectors[..., half_dim:]
    return jnp.concatenate([lower_half * cos_t - upper_half * sin_t, upper_half * cos_t + lower_half * sin_t], axis=-1)


def project_token(hidden, w_norm, w_q, w_k, w_v, cache_len):
    head_dim = w_k.shape[1]
    num_heads = w_q.shape[1] // head_dim
    num_rows = hidden.shape[0]
    x_f32 = hidden.astype(jnp.float32)
    inv_rms = lax.rsqrt(jnp.mean(x_f32 * x_f32, axis=-1, keepdims=True) + EPSILON)
    x_norm = (x_f32 * inv_rms * (1.0 + w_norm.astype(jnp.float32))).astype(jnp.bfloat16)
    q_proj = jnp.dot(x_norm, w_q, preferred_element_type=jnp.float32).astype(jnp.bfloat16)
    k_proj = jnp.dot(x_norm, w_k, preferred_element_type=jnp.float32).astype(jnp.bfloat16)
    v_proj = jnp.dot(x_norm, w_v, preferred_element_type=jnp.float32).astype(jnp.bfloat16)
    inv_freq = ROPE_BASE ** (-jnp.arange(head_dim // 2, dtype=jnp.float32) * 2.0 / head_dim)
    angles = cache_len.astype(jnp.float32)[:, None] * inv_freq[None, :]
    cos_t = jnp.cos(angles)
    sin_t = jnp.sin(angles)
    q_heads = q_proj.astype(jnp.float32).reshape(num_rows, num_heads, head_dim)
    q_rot = (rotate_half(q_heads, cos_t[:, None, :], sin_t[:, None, :]) * head_dim ** -0.5).astype(jnp.bfloat16)
    k_rot = rotate_half(k_proj.astype(jnp.float32), cos_t, sin_t).astype(jnp.bfloat16)
    return x_f32, q_rot, k_rot, v_proj


def local_step(hidden, w_norm, w_q, w_k, w_v, w_o, k_block, v_block, cache_len):
    num_rows = hidden.shape[0]
    seq_block = k_block.shape[1]
    x_f32, q_rot, k_rot, v_proj = project_token(hidden, w_norm, w_q, w_k, w_v, cache_len)
    positions = lax.axis_index('sp') * seq_block + jnp.arange(seq_block)
    at_slot = (positions[None, :] == cache_len[:, None])[:, :, None]
    new_k_block = jnp.where(at_slot, k_rot[:, None, :], k_block)
    new_v_block = jnp.where(at_slot, v_proj[:, None, :], v_block)
    is_valid = (positions[None, :] <= cache_len[:, None])[:, None, :]
    scores = jnp.einsum('rhd,rtd->rht', q_rot, new_k_block, preferred_element_type=jnp.float32)
    masked = jnp.where(is_valid, scores, -jnp.inf)
    row_max = lax.pmax(jnp.max(masked, axis=-1), 'sp')
    weights = jnp.exp(masked - row_max[:, :, None])
    part_num = jnp.einsum('rht,rtd->rhd', weights.astype(jnp.bfloat16), new_v_block, preferred_element_type=jnp.float32)
    part_den = jnp.sum(weights, axis=-1)
    numerator, denominator = lax.psum((part_num, part_den), 'sp')
    attended = (numerator / denominator[:, :, None]).astype(jnp.bfloat16).reshape(num_rows, -1)
    out_hidden = x_f32 + jnp.dot(attended, w_o, preferred_element_type=jnp.float32)
    return out_hidden.astype(jnp.bfloat16), new_k_block, new_v_block


def solution(mesh):
    cache_spec = P('dp', 'sp', None)
    return jax.shard_map(local_step, mesh=mesh, in_specs=(P('dp', None), P(None), P(None, None), P(None, None), P(None, None), P(None, None), cache_spec, cache_spec, P('dp')), out_specs=(P('dp', None), cache_spec, cache_spec), check_vma=False)
```

profile of v0, /device:TPU:81, one launch (start us, length us, event | category | flops | bytes accessed | tf_op | source)
XLA Modules:
  0.0 156.2 jit_solution(13166642747486016752)
XLA Ops:
  7.2 0.0 copy-start
  7.2 0.1 all-reduce.2.cloned.1.call-start
  7.3 0.8 convert_element_type.46
  8.1 1.5 fusion.2
  9.6 0.0 copy-start.3
  9.6 0.0 copy-start.4
  9.6 0.9 convert_add_fusion
  10.5 0.8 broadcast_compare_fusion.1
  11.3 0.0 copy-done
  11.3 1.7 %convolution_convert_fusion.1 = bf16[128,256]{1,0:T(8,128)(2,1)S(1)} fusion(bf16[4096,256]{1,0:T(8,128)(2,1)S(1)} %copy-done, bf16[128,4096]{1,0:T(8,128)(2,1)} %param.9, f32[4096]{0:T(1024)S(1)} %convert_add_fusion, f32[128]{0:T(128)S(1)} %add_rsqrt_fusion), kind=kOutput, calls=%fused_computation.15 | convolution fusion | flops 270565376 | bytes 3228160 | tf_op jit(solution)/shard_map/dot_general | solution.py:26
  13.0 0.0 copy-done.3
  13.1 0.0 copy-done.4
  13.1 0.5 fusion.6
  13.6 13.0 %fusion.1 = f32[128,4096]{1,0:T(8,128)S(1)} fusion(bf16[4096,4096]{1,0:T(8,128)(2,1)} %param.11, bf16[128,4096]{1,0:T(8,128)(2,1)S(1)} %copy-done.3, f32[4096]{0:T(1024)S(1)} %convert_add_fusion, f32[128]{0:T(128)S(1)} %add_rsqrt_fusion), kind=kOutput, calls=%fused_computation.5 | convolution fusion | flops 4298113024 | bytes 36717056 | tf_op jit(solution)/shard_map/dot_general | solution.py:24
  26.5 0.7 copy.12
  27.2 0.3 multiply_cosine_fusion
  27.5 0.3 multiply_subtract_fusion
  27.8 9.8 %broadcast_select_fusion.1 = (bf16[128,128,256]{2,1,0:T(8,128)(2,1)S(1)}, bf16[128,128,256]{2,1,0:T(8,128)(2,1)}) fusion(bf16[128,128,256]{2,1,0:T(8,128)(2,1)} %param.15, pred[128,128]{1,0:T(8,128)(4,1)S(1)} %get-tuple-element.10, bf16[128,256]{1,0:T(8,128)(2,1)S(1)} %pad_maximum_fusion, bf16[128,128,256]{2,1,0:T(8,128)(2,1)} %param.16, ...), kind=kLoop, calls=%fused_computation.1 | loop fusion | flops 8388608 | bytes 33701888 | tf_op jit(solution)/shard_map/jit(_where)/select_n | solution.py:43
  37.6 0.0 copy-start.2
  37.6 2.4 %fusion.19 = (f32[128,16]{1,0:T(8,128)S(1)}, f32[128,16,128]{2,1,0:T(8,128)S(1)}) fusion(bf16[128,128,256]{2,1,0:T(8,128)(2,1)S(1)} %get-tuple-element.7, f32[128,16,128]{2,1,0:T(8,128)S(1)} %get-tuple-element.4, f32[128,16,128]{2,1,0:T(8,128)S(1)} %get-tuple-element.3, pred[128,128]{1,0:T(8,128)(4,1)S(1)} %get-tuple-element.9), kind=kOutput, calls=%fused_computation.39 | convolution fusion | flops 136312832 | bytes 11558912 | tf_op jit(solution)/shard_map/rhd,rtd->rht/dot_general | solution.py:46
  40.0 1.0 copy-done.2
  41.0 24.4 %pmax.7 = f32[128,16]{1,0:T(8,128)S(1)} all-reduce(f32[128,16]{1,0:T(8,128)S(1)} %get-tuple-element.15), channel_id=1, replica_groups=mesh['dp'=4,'sp'=8] {'sp'}, use_global_device_ids=true, to_apply=%region_2.3 | all-reduce | flops 2048 | bytes 16384 | tf_op jit(solution)/shard_map/pmax | solution.py:48
  65.4 5.9 %fusion.11 = f32[128,16,256]{2,1,0:T(8,128)} fusion(bf16[128,128,256]{2,1,0:T(8,128)(2,1)} %get-tuple-element.8, f32[128,16,128]{2,1,0:T(8,128)S(1)} %get-tuple-element.16, f32[128,16]{1,0:T(8,128)S(1)} %pmax.7), kind=kOutput, calls=%fused_computation.24 | convolution fusion | flops 134742016 | bytes 11542528 | tf_op jit(solution)/shard_map/rht,rtd->rhd/dot_general | solution.py:50
  71.4 0.1 all-reduce.2.cloned.1.call-update
  71.5 0.7 fusion.9
  72.1 25.4 %psum.15 = f32[128,16]{1,0:T(8,128)S(1)} all-reduce(f32[128,16]{1,0:T(8,128)S(1)} %fusion.9), channel_id=1, replica_groups=mesh['dp'=4,'sp'=8] {'sp'}, use_global_device_ids=true, to_apply=%region_5.6 | all-reduce | flops 2048 | bytes 16384 | tf_op jit(solution)/shard_map/psum | solution.py:52
  97.5 35.2 %all-reduce.2.cloned.1.call-done = f32[128,16,256]{2,1,0:T(8,128)} async-done(((f32[128,16,256]{2,1,0:T(8,128)}), f32[128,16,256]{2,1,0:T(8,128)}) %all-reduce.2.cloned.1.call-update) | async-done | bytes 2097168 | tf_op jit(solution)/shard_map/psum | solution.py:52
  132.7 1.9 %divide_convert_fusion = bf16[128,16,256]{2,1,0:T(8,128)(2,1)S(1)} fusion(f32[128,16,256]{2,1,0:T(8,128)} %all-reduce.2.cloned.1.call-done, f32[128,16]{1,0:T(8,128)S(1)} %psum.15), kind=kLoop, calls=%fused_computation.13 | loop fusion | flops 1048576 | bytes 3153920 | tf_op jit(solution)/shard_map/convert_element_type | solution.py:53
  134.7 0.4 copy.13
  135.1 0.0 copy-start.1
  135.1 14.2 %fusion = bf16[128,4096]{1,0:T(8,128)(2,1)} fusion(bf16[128,4096]{1,0:T(8,128)(2,1)S(1)} %bitcast.13, bf16[4096,4096]{1,0:T(8,128)(2,1)} %param.14, bf16[128,4096]{1,0:T(8,128)(2,1)S(1)} %copy-done.3), kind=kOutput, calls=%fused_computation.3 | convolution fusion | flops 4296540160 | bytes 36700160 | tf_op jit(solution)/shard_map/dot_general | solution.py:54
  149.4 0.0 copy-done.1
  (4 shorter events, 0.0 us)
Async XLA Ops:
  7.2 4.1 %copy-start = (bf16[4096,256]{1,0:T(8,128)(2,1)S(1)}, bf16[4096,256]{1,0:T(8,128)(2,1)}, u32[]{:S(2)}) copy-start(bf16[4096,256]{1,0:T(8,128)(2,1)} %param.13) | copy-start | bytes 6291460
  7.2 125.5 %all-reduce.2.cloned.1.call-start = ((), (), s32[]{:S(2)}) async-start(), calls=%async_computation | async-start | bytes 4194304 | tf_op jit(solution)/shard_map/psum | solution.py:52
  9.6 3.4 %copy-start.3 = (bf16[128,4096]{1,0:T(8,128)(2,1)S(1)}, bf16[128,4096]{1,0:T(8,128)(2,1)}, u32[]{:S(2)}) copy-start(bf16[128,4096]{1,0:T(8,128)(2,1)} %param.9) | copy-start | bytes 3145732
  9.6 3.5 %copy-start.4 = (bf16[4096,256]{1,0:T(8,128)(2,1)S(1)}, bf16[4096,256]{1,0:T(8,128)(2,1)}, u32[]{:S(2)}) copy-start(bf16[4096,256]{1,0:T(8,128)(2,1)} %param.12) | copy-start | bytes 6291460
  37.6 3.4 %copy-start.2 = (bf16[128,128,256]{2,1,0:T(8,128)(2,1)}, bf16[128,128,256]{2,1,0:T(8,128)(2,1)S(1)}, u32[]{:S(2)}) copy-start(bf16[128,128,256]{2,1,0:T(8,128)(2,1)S(1)} %get-tuple-element.7) | copy-start | bytes 25165828
  135.1 14.3 %copy-start.1 = (bf16[4096,256]{1,0:T(8,128)(2,1)S(1)}, bf16[4096,256]{1,0:T(8,128)(2,1)}, u32[]{:S(2)}) copy-start(bf16[4096,256]{1,0:T(8,128)(2,1)} %param.13) | copy-start | bytes 6291460
Sparse Core Ops, SparseCore 0:
  71.6 61.1 all-reduce.1
where the time goes:
time: 157 us; the launch traced here: 156 us
  blocking collectives  49.8 us (32%)
  matrix products  37.7 us (24%)
  waiting for transfers between devices  35.3 us (22%)
  other arithmetic  17 us (11%)
  between operations  14.2 us (9%)
  local copies, waits for them, and re-layouts  2.16 us (1%)
    psum x1, waiting for transfers between devices, local_step(): numerator, denominator = lax.psum((part_num, part_den), 'sp')  35.2 us
    psum x1, blocking collectives, local_step(): numerator, denominator = lax.psum((part_num, part_den), 'sp')  25.4 us
    pmax x1, blocking collectives, local_step(): row_max = lax.pmax(jnp.max(masked, axis=-1), 'sp')  24.4 us
    dot_general x1, matrix products, local_step(): jnp.dot(attended, w_o, preferred_element_type=jnp.float32)  14.2 us
    dot_general x1, matrix products, project_token(): jnp.dot(x_norm, w_q, preferred_element_type=jnp.float32)  13 us
    select_n x1, other arithmetic, local_step(): new_k_block = jnp.where(at_slot, k_rot[:, None, :], k_block)  9.75 us
    dot_general x1, matrix products, local_step(): jnp.einsum('rht,rtd->rhd', weights.astype(jnp.bfloat16), new_v_block, pre...  5.95 us
  transfers between devices with their start and end apart: 1, of which 1 were waited for; matrix products, arithmetic and copies ran while one was open for 0% of the time, Pallas kernels for 0%

commit v1 on v0

v1 whole, which is shorter than its diff:
```python
import functools

import jax
import jax.numpy as jnp
from jax import lax
from jax.experimental import pallas as pl
from jax.experimental.pallas import tpu as pltpu
from jax.sharding import PartitionSpec as P

ROPE_BASE = 10000.0
EPSILON = 1e-6
MESH = pl.DeviceIdType.MESH
MIB = 1 << 20
LOWEST = float(jnp.finfo(jnp.float32).min)
CHIPS = 4


def rotate(x, cos_t, sin_t):
    half = x.shape[-1] // 2
    low, high = x[:, :half], x[:, half:]
    return jnp.concatenate([low * cos_t - high * sin_t, high * cos_t + low * sin_t], axis=-1)


def project_kernel(hid_ref, wn_ref, cos_ref, sin_ref, wk_hbm, wv_hbm, wq_hbm, q_ref, k_ref, v_ref,
                   xn, wk, wv, wq, sem_k, sem_v, sem_q):
    rows, head_dim = hid_ref.shape[0], wk.shape[1]
    heads, half = wq.shape[0], head_dim // 2
    brows = rows // q_ref.shape[0]
    core = lax.rem(lax.axis_index('sp'), 2)

    def q_copy(j):
        columns = pl.ds(pl.multiple_of((core * heads + j) * head_dim, head_dim), head_dim)
        return pltpu.make_async_copy(wq_hbm.at[:, columns], wq.at[j], sem_q.at[j])

    k_copy = pltpu.make_async_copy(wk_hbm, wk, sem_k)
    v_copy = pltpu.make_async_copy(wv_hbm, wv, sem_v)
    k_copy.start()
    v_copy.start()
    for j in range(heads):
        q_copy(j).start()
    x = hid_ref[...].astype(jnp.float32)
    inv_rms = lax.rsqrt(jnp.mean(x * x, axis=-1, keepdims=True) + EPSILON)
    xn[...] = (x * inv_rms * (1.0 + wn_ref[...].astype(jnp.float32))).astype(jnp.bfloat16)
    cos_t, sin_t = cos_ref[...], sin_ref[...]

    def project(w):
        y = jnp.dot(xn[...], w, preferred_element_type=jnp.float32)
        return y.astype(jnp.bfloat16)

    k_copy.wait()
    k_ref[...] = rotate(project(wk[...]).astype(jnp.float32), cos_t, sin_t).astype(jnp.bfloat16)
    v_copy.wait()
    v_ref[...] = project(wv[...])

    def one_head(j, carry):
        q_copy(j).wait()
        y = project(wq[j]).astype(jnp.float32)
        y = (rotate(y, cos_t, sin_t) * head_dim ** -0.5).astype(jnp.bfloat16).astype(jnp.float32)
        for i in range(q_ref.shape[0]):
            for d in range(2):
                q_ref[i, d, pl.ds(j, brows, stride=heads), :] = y[i * brows:(i + 1) * brows, d * half:(d + 1) * half]
        return carry

    lax.fori_loop(0, heads, one_head, 0)


def attend_kernel(len_ref, qh_ref, kc_ref, vc_ref, hid_ref, wo_hbm, out_ref,
                  q_all, p_buf, num, stat_src, stat_dst, d_recv, s_sum, r_recv, l_recv, from_left, from_right,
                  att, a_bf, wo, gath, other,
                  sem_wo, sem_ql, q_s, q_r, st_s, st_r, d_s, d_r, rs_s, rs_r, at_s, at_r,
                  own_s, own_r, fw_s, fw_r, h_s, h_r):
    f32, bf16 = jnp.float32, jnp.bfloat16
    me = lax.axis_index('sp')
    chip, core = me // 2, lax.rem(me, 2)
    mate = 1 - core
    peers = 2 * CHIPS
    slots = kc_ref.shape[1]
    nblk, brows = num.shape[0], kc_ref.shape[0] // num.shape[0]
    heads = num.shape[2] // brows
    hh = heads // 2
    hl = num.shape[3]
    hd = 2 * hl
    nq = wo.shape[0]

    def at(c, k):
        return {'sp': lax.rem(c + CHIPS, CHIPS) * 2 + k}

    right, left = at(chip + 1, core), at(chip - 1, core)
    partner = at(chip, mate)

    def remote(src, dst, ssem, rsem, dev):
        return pltpu.make_async_remote_copy(src_ref=src, dst_ref=dst, send_sem=ssem, recv_sem=rsem,
                                            device_id=dev, device_id_type=MESH)

    def wo_copy(j):
        columns = pl.ds(pl.multiple_of((core * nq + j) * hd, hd), hd)
        return pltpu.make_async_copy(wo_hbm.at[:, columns], wo.at[j], sem_wo.at[j])

    for j in range(nq):
        wo_copy(j).start()

    barrier = pltpu.get_barrier_semaphore()
    for d in range(1, peers):
        pl.semaphore_signal(barrier, inc=1, device_id={'sp': lax.rem(me + d, peers)}, device_id_type=MESH)
    pl.semaphore_wait(barrier, peers - 1)

    nqc = q_s.shape[0]
    per = nblk // nqc
    q_sends, q_local = [], []
    for t in range(nqc):
        part = pl.ds(t * per, per)
        copy = remote(qh_ref.at[part], q_all.at[core, part], q_s.at[t], q_r.at[t], partner)
        copy.start()
        q_sends.append(copy)
        copy = pltpu.make_async_copy(qh_ref.at[part], q_all.at[core, part], sem_ql.at[t])
        copy.start()
        q_local.append(copy)

    lane = lax.broadcasted_iota(jnp.int32, (heads, slots), 1)
    position = me * slots + lane

    def scores(i, kk):
        c = i // 2
        stat = stat_src[kk]
        base = c * brows
        for r in range(brows):
            b = i * brows + r
            own_rows = slice(r * hh, (r + 1) * hh)
            q = jnp.concatenate([
                jnp.concatenate([q_all[k, i, d, own_rows, :] for k in range(2)], axis=0) for d in range(2)], axis=1)
            s = lax.dot_general(q.astype(bf16), kc_ref[b], (((1,), (1,)), ((), ())), preferred_element_type=f32)
            valid = position <= len_ref[b]
            s = jnp.where(valid, s, LOWEST)
            m = jnp.max(s, axis=1, keepdims=True)
            p = jnp.where(valid, jnp.exp(s - m), 0.0)
            p_buf[b] = p.astype(bf16)
            den = jnp.sum(p, axis=1, keepdims=True)
            stat = jnp.where(lane == base + r, m, jnp.where(lane == slots // 2 + base + r, den, stat))
        stat_src[kk] = stat

    stat_src[...] = jnp.zeros_like(stat_src)
    for t in range(nqc):
        q_local[t].wait()
        q_sends[t].wait_recv()

        def pair(u, carry):
            i = t * per + u
            scores(i, lax.rem(i, 2))
            return carry

        lax.fori_loop(0, per, pair, 0)

    st_sends = []
    for d in range(1, peers):
        target = lax.rem(me + d, peers)
        copy = remote(stat_src.at[lax.rem(target, 2)], stat_dst.at[d - 1], st_s.at[d - 1], st_r.at[d - 1],
                      {'sp': target})
        copy.start()
        st_sends.append(copy)

    def values(i):
        for r in range(brows):
            b = i * brows + r
            o = jnp.dot(p_buf[b], vc_ref[b], preferred_element_type=f32)
            for d in range(2):
                num[i, d, r * heads:(r + 1) * heads, :] = o[:, d * hl:(d + 1) * hl]

    offsets = (2, 1, 3, 0)
    places = [lax.rem(chip + o, CHIPS) for o in offsets]
    d_sends = []
    for t in range(CHIPS):
        values(2 * places[t] + mate)
        copy = remote(num.at[2 * places[t] + mate], d_recv.at[t], d_s.at[t], d_r.at[t], partner)
        copy.start()
        d_sends.append(copy)
        values(2 * places[t] + core)

    for copy in st_sends:
        copy.wait_recv()
    mine = stat_src[core]
    theirs = [stat_dst[d] for d in range(peers - 1)]
    top = functools.reduce(jnp.maximum, theirs, mine)
    half = slots // 2
    mate_d = jnp.where(core == 1, 0, peers - 2)
    own_a = jnp.exp(mine - top)
    total = own_a * pltpu.roll(mine, half, 1)
    for x in theirs:
        total = total + jnp.exp(x - top) * pltpu.roll(x, half, 1)
    in_use = lane < half
    total = jnp.where(in_use, total, 1.0)
    f_own = jnp.where(in_use, own_a, 0.0) / total
    f_mate = jnp.where(in_use, jnp.exp(stat_dst[mate_d] - top), 0.0) / total

    def combine(t):
        d_sends[t].wait_recv()
        shift = slots - places[t] * brows
        fo, fm = pltpu.roll(f_own, shift, 1), pltpu.roll(f_mate, shift, 1)
        i = 2 * places[t] + core
        for r in range(brows):
            part = pl.ds(r * heads, heads)
            for d in range(2):
                s_sum[t, d, part, :] = num[i, d, part, :] * fo[:, r:r + 1] + d_recv[t, d, part, :] * fm[:, r:r + 1]

    def ring(n, src, dst, dev):
        copy = remote(src, dst, rs_s.at[n], rs_r.at[n], dev)
        copy.start()
        return copy

    combine(0)
    r1 = ring(0, s_sum.at[0, 0], r_recv, right)
    l1 = ring(1, s_sum.at[0, 1], l_recv, left)
    combine(1)
    r2a = ring(2, s_sum.at[1, 1], from_left.at[1], right)
    combine(2)
    l2a = ring(3, s_sum.at[2, 0], from_right.at[0], left)
    r1.wait_recv()
    s_sum[1, 0] = s_sum[1, 0] + r_recv[...]
    r2b = ring(4, s_sum.at[1, 0], from_left.at[0], right)
    l1.wait_recv()
    s_sum[2, 1] = s_sum[2, 1] + l_recv[...]
    l2b = ring(5, s_sum.at[2, 1], from_right.at[1], left)
    combine(3)
    for copy in (r2a, r2b, l2a, l2b):
        copy.wait_recv()
    att[core] = s_sum[3] + from_left[...] + from_right[...]
    at_copy = remote(att.at[core], att.at[core], at_s, at_r, partner)
    at_copy.start()
    at_copy.wait_recv()

    for h in range(heads):
        for d in range(2):
            pair = [att[kk, d, pl.ds(h, brows, stride=heads), :] for kk in range(2)]
            a_bf[:, h * hd + d * hl:h * hd + (d + 1) * hl] = jnp.concatenate(pair, axis=0).astype(bf16)
    crow = 2 * brows

    def own_copies(n):
        piece = gath.at[chip, n]
        return (remote(piece, piece, own_s.at[0, n], own_r.at[0, n], right),
                remote(piece, piece, own_s.at[1, n], own_r.at[1, n], left),
                remote(piece, other.at[chip, n], h_s.at[0, n], h_r.at[0, n], partner))

    def rows_of(c):
        return pl.ds(pl.multiple_of(c * crow, crow), crow)

    def columns_of(k, n):
        return pl.ds(pl.multiple_of((k * nq + n) * hd, hd), hd)

    def project(n, carry):
        wo_copy(n).wait()
        y = jnp.dot(a_bf[...], wo[n], preferred_element_type=f32)
        x = hid_ref[rows_of(chip), columns_of(core, n)].astype(f32)
        gath[chip, n] = x + y
        for copy in own_copies(n):
            copy.start()
        return carry

    lax.fori_loop(0, nq, project, 0)

    cl, cr, co = places[2], places[1], places[0]
    fsplit = nq // 2

    def forward(n):
        if n < fsplit:
            return remote(gath.at[cl, n], gath.at[cl, n], fw_s.at[n], fw_r.at[n], right)
        return remote(gath.at[cr, n], gath.at[cr, n], fw_s.at[n], fw_r.at[n], left)

    def to_mate(which, c, n):
        return remote(gath.at[c, n], other.at[c, n], h_s.at[which, n], h_r.at[which, n], partner)

    def put(c, n):
        out_ref[rows_of(c), columns_of(core, n)] = gath[c, n].astype(bf16)

    for n in range(nq):
        from_l, from_r, _ = own_copies(n)
        from_l.wait_recv()
        if n < fsplit:
            forward(n).start()
        to_mate(1, cl, n).start()
        from_r.wait_recv()
        if n >= fsplit:
            forward(n).start()
        to_mate(2, cr, n).start()
    for n in range(nq):
        put(chip, n)
        put(cl, n)
        put(cr, n)
    for n in range(nq):
        forward(n).wait_recv()
        to_mate(3, co, n).start()
        put(co, n)
    for which, c in enumerate((chip, cl, cr, co)):
        for n in range(nq):
            to_mate(which, c, n).wait_recv()
            out_ref[rows_of(c), columns_of(mate, n)] = other[c, n].astype(bf16)

    for copy in q_sends + st_sends + d_sends + [r1, l1, r2a, l2a, r2b, l2b, at_copy]:
        copy.wait_send()
    for n in range(nq):
        for copy in own_copies(n):
            copy.wait_send()
        forward(n).wait_send()
        for which, c in ((1, cl), (2, cr), (3, co)):
            to_mate(which, c, n).wait_send()


def local_step(hidden, w_norm, w_q, w_k, w_v, w_o, k_block, v_block, cache_len):
    f32, bf16 = jnp.float32, jnp.bfloat16
    rows, width = hidden.shape
    seq_block, hd = k_block.shape[1], k_block.shape[2]
    heads = w_q.shape[1] // hd
    hh = heads // 2
    nblk = 2 * CHIPS
    brows = rows // nblk
    inv_freq = ROPE_BASE ** (-jnp.arange(hd // 2, dtype=f32) * 2.0 / hd)
    angles = cache_len.astype(f32)[:, None] * inv_freq[None, :]
    cos_t, sin_t = jnp.cos(angles), jnp.sin(angles)
    vmem = pl.BlockSpec(memory_space=pltpu.VMEM)
    hbm = pl.BlockSpec(memory_space=pl.ANY)
    smem = pl.BlockSpec(memory_space=pltpu.SMEM)
    dma = pltpu.SemaphoreType.DMA

    qh, k_rot, v_new = pl.pallas_call(
        project_kernel,
        out_shape=(jax.ShapeDtypeStruct((nblk, 2, brows * hh, hd // 2), f32), jax.ShapeDtypeStruct((rows, hd), bf16),
                   jax.ShapeDtypeStruct((rows, hd), bf16)),
        in_specs=[vmem] * 4 + [hbm] * 3,
        out_specs=(vmem,) * 3,
        scratch_shapes=[
            pltpu.VMEM((rows, width), bf16),
            pltpu.VMEM((width, hd), bf16),
            pltpu.VMEM((width, hd), bf16),
            pltpu.VMEM((hh, width, hd), bf16),
            dma, dma, dma((hh,)),
        ],
        compiler_params=pltpu.CompilerParams(vmem_limit_bytes=28 * MIB),
        cost_estimate=pl.CostEstimate(flops=2 * rows * width * (hh + 2) * hd, bytes_accessed=2 * width * (hh + 2) * hd,
                                      transcendentals=0),
        name='project',
    )(hidden, w_norm.reshape(1, width), cos_t, sin_t, w_k, w_v, w_q)

    positions = lax.axis_index('sp') * seq_block + jnp.arange(seq_block)
    at_slot = (positions[None, :] == cache_len[:, None])[:, :, None]
    new_k_block = jnp.where(at_slot, k_rot[:, None, :], k_block)
    new_v_block = jnp.where(at_slot, v_new[:, None, :], v_block)

    block, hl = brows * heads, hd // 2
    nqc = CHIPS
    out_hidden = pl.pallas_call(
        attend_kernel,
        out_shape=jax.ShapeDtypeStruct((rows, width), bf16),
        in_specs=[smem, vmem, vmem, vmem, vmem, hbm],
        out_specs=vmem,
        scratch_shapes=[
            pltpu.VMEM((2, nblk, 2, brows * hh, hl), f32),
            pltpu.VMEM((rows, heads, seq_block), bf16),
            pltpu.VMEM((nblk, 2, block, hl), f32),
            pltpu.VMEM((2, heads, seq_block), f32),
            pltpu.VMEM((nblk - 1, heads, seq_block), f32),
            pltpu.VMEM((CHIPS, 2, block, hl), f32),
            pltpu.VMEM((CHIPS, 2, block, hl), f32),
            pltpu.VMEM((block, hl), f32),
            pltpu.VMEM((block, hl), f32),
            pltpu.VMEM((2, block, hl), f32),
            pltpu.VMEM((2, block, hl), f32),
            pltpu.VMEM((2, 2, block, hl), f32),
            pltpu.VMEM((2 * brows, width), bf16),
            pltpu.VMEM((hh, width, hd), bf16),
            pltpu.VMEM((CHIPS, hh, 2 * brows, hd), f32),
            pltpu.VMEM((CHIPS, hh, 2 * brows, hd), f32),
            dma((hh,)), dma((nqc,)), dma((nqc,)), dma((nqc,)), dma((nblk - 1,)), dma((nblk - 1,)),
            dma((CHIPS,)), dma((CHIPS,)), dma((6,)), dma((6,)), dma, dma,
            dma((2, hh)), dma((2, hh)), dma((hh,)), dma((hh,)), dma((CHIPS, hh)), dma((CHIPS, hh)),
        ],
        compiler_params=pltpu.CompilerParams(collective_id=0, has_side_effects=True, vmem_limit_bytes=34 * MIB),
        cost_estimate=pl.CostEstimate(flops=2 * rows * width * hh * hd * 2, bytes_accessed=2 * width * hh * hd,
                                      transcendentals=0),
        name='attend',
    )(cache_len, qh, new_k_block, new_v_block, hidden, w_o)
    return out_hidden, new_k_block, new_v_block


def solution(mesh):
    assert mesh.shape['sp'] == 2 * CHIPS
    cache_spec = P('dp', 'sp', None)
    return jax.shard_map(local_step, mesh=mesh, in_specs=(P('dp', None), P(None), P(None, None), P(None, None), P(None, None), P(None, None), cache_spec, cache_spec, P('dp')), out_specs=(P('dp', None), cache_spec, cache_spec), check_vma=False)
```

time: 157 us -> 63 us (0.40)
  blocking collectives: 49.8 us -> 0 us
  Pallas kernels: 0 us -> 47.6 us
  matrix products: 37.7 us -> 0 us
  waiting for transfers between devices: 35.3 us -> 0 us
  between operations: 14.2 us -> 0.74 us
  other arithmetic: 17 us -> 7.07 us
  local copies, waits for them, and re-layouts: 2.16 us -> 7.26 us
    pallas_call x0 -> x2, Pallas kernels: none -> 47.6 us  [the longest x1 40.4 us: local_step(): pl.pallas_call(attend_kernel, out_shape=jax.ShapeDtypeStruct((rows, width...]
    dot_general x6 -> x0, matrix products: 37.7 us -> none  [the longest x1 14.2 us: local_step(): jnp.dot(attended, w_o, preferred_element_type=jnp.float32)]
    psum x1 -> x0, waiting for transfers between devices: 35.2 us -> none  [local_step(): numerator, denominator = lax.psum((part_num, part_den), 'sp')]
    psum x1 -> x0, blocking collectives: 25.4 us -> none  [local_step(): numerator, denominator = lax.psum((part_num, part_den), 'sp')]
    pmax x1 -> x0, blocking collectives: 24.4 us -> none  [local_step(): row_max = lax.pmax(jnp.max(masked, axis=-1), 'sp')]
    select_n x1, other arithmetic: 9.75 us -> 5.35 us  [local_step(): new_v_block = jnp.where(at_slot, v_new[:, None, :], v_block)]
    unnamed x12 -> x17, local copies, waits for them, and re-layouts: 2.16 us -> 6.55 us
    reduce_sum x2 -> x0, other arithmetic: 2.18 us -> none  [the longest x1 1.52 us: project_token(): jnp.mean(x_f32 * x_f32, axis=-1, keepdims=True) + EPSILON]
  transfers between devices with their start and end apart: 1 -> 0, of which waited for: 1 -> 0; matrix products, arithmetic and copies ran while one was open for 0% -> 0% of each run, Pallas kernels for 0% -> 0%
where the time goes in v1:
time: 63 us; the launch traced here: 62.7 us
  Pallas kernels  47.6 us (76%)
  local copies, waits for them, and re-layouts  7.26 us (12%)
  other arithmetic  7.07 us (11%)
  between operations  0.74 us (1%)
    pallas_call x1, Pallas kernels, local_step(): pl.pallas_call(attend_kernel, out_shape=jax.ShapeDtypeStruct((rows, width...  40.4 us
    pallas_call x1, Pallas kernels, local_step(): pl.pallas_call(project_kernel, out_shape=(jax.ShapeDtypeStruct((nblk, 2,...  7.2 us
    unnamed x17, local copies, waits for them, and re-layouts  6.55 us
    select_n x1, other arithmetic, local_step(): new_v_block = jnp.where(at_slot, v_new[:, None, :], v_block)  5.35 us

profile of v1, /device:TPU:81, one launch (start us, length us, event | category | flops | bytes accessed | tf_op | source)
XLA Modules:
  0.0 62.7 jit_solution(878800287533634733)
XLA Ops:
  0.6 0.7 %convert_element_type.3 = f32[128]{0:T(128)S(1)} convert(s32[128]{0:T(128)} %len_ref.1) | non-fusion elementwise | flops 128 | bytes 1024 | tf_op jit(solution)/shard_map/convert_element_type | solution.py:315
  1.3 0.7 %broadcast_compare_fusion = pred[128,128]{1,0:T(8,128)(4,1)S(1)} fusion(s32[128]{0:T(128)S(1)} %iota_add_fusion, s32[128]{0:T(128)} %len_ref.1), kind=kLoop, calls=%fused_computation.4 | loop fusion | flops 16384 | bytes 17408 | tf_op jit(solution)/shard_map/eq | solution.py:342
  2.1 0.7 %reshape.50.wn_ref = bf16[1,4096]{1,0:T(2,128)(2,1)S(1)} reshape(bf16[4096]{0:T(1024)(128)(2,1)} %param.10) | data formatting | bytes 16384 | tf_op jit(solution)/shard_map/reshape | solution.py:339
  2.8 0.3 multiply_sine_fusion
  3.1 0.0 copy-start.2
  3.1 1.2 %copy-done.2 = bf16[128,4096]{1,0:T(8,128)(2,1)S(1)} copy-done((bf16[128,4096]{1,0:T(8,128)(2,1)S(1)}, bf16[128,4096]{1,0:T(8,128)(2,1)}, u32[]{:S(2)}) %copy-start.2) | copy-done | bytes 1048600
  4.3 0.0 copy-start.4
  4.3 1.6 %copy-done.4 = bf16[4096,256]{1,0:T(8,128)(2,1)S(1)} copy-done((bf16[4096,256]{1,0:T(8,128)(2,1)S(1)}, bf16[4096,256]{1,0:T(8,128)(2,1)}, u32[]{:S(2)}) %copy-start.4) | copy-done | bytes 2097176
  5.9 0.0 copy-start.5
  5.9 1.6 %copy-done.5 = bf16[4096,256]{1,0:T(8,128)(2,1)S(1)} copy-done((bf16[4096,256]{1,0:T(8,128)(2,1)S(1)}, bf16[4096,256]{1,0:T(8,128)(2,1)}, u32[]{:S(2)}) %copy-start.5) | copy-done | bytes 2097176
  7.5 0.0 copy-start.7
  7.5 7.2 %project.1 = (f32[8,2,128,128]{3,2,1,0:T(8,128)S(1)}, bf16[128,256]{1,0:T(8,128)(2,1)S(1)}, bf16[128,256]{1,0:T(8,128)(2,1)S(1)}) custom-call(bf16[128,4096]{1,0:T(8,128)(2,1)S(1)} %copy-done.2, bf16[1,4096]{1,0:T(2,128)(2,1)S(1)} %reshape.50.wn_ref, f32[128,128]{1,0:T(8,128)S(1)} %get-tuple-element.12.cos_ref, f32[128,128]{1,0:T(8,128)S(1)} %get-tuple-element.11.sin_ref, ...), custom_call_target="tpu_custom_call" | custom-call | flops 2684354560 | bytes 20971520 | tf_op jit(solution)/shard_map/project/pallas_call | solution.py:322
  14.7 1.1 %copy-done.7 = bf16[128,128,256]{2,1,0:T(8,128)(2,1)S(1)} copy-done((bf16[128,128,256]{2,1,0:T(8,128)(2,1)S(1)}, bf16[128,128,256]{2,1,0:T(8,128)(2,1)}, u32[]{:S(2)}) %copy-start.7) | copy-done | bytes 8388632
  15.9 0.0 copy-start.3
  15.9 0.0 copy-start.6
  15.9 5.4 %broadcast_select_fusion = (bf16[128,128,256]{2,1,0:T(8,128)(2,1)S(1)}, bf16[128,128,256]{2,1,0:T(8,128)(2,1)S(1)}) fusion(bf16[128,128,256]{2,1,0:T(8,128)(2,1)S(1)} %copy-done.7, pred[128,128]{1,0:T(8,128)(4,1)S(1)} %broadcast_compare_fusion, bf16[128,256]{1,0:T(8,128)(2,1)S(1)} %get-tuple-element.8, bf16[128,128,256]{2,1,0:T(8,128)(2,1)} %param.15, ...), kind=kLoop, calls=%fused_computation | loop fusion | flops 8388608 | bytes 33701888 | tf_op jit(solution)/shard_map/jit(_where)/select_n | solution.py:344
  21.2 0.0 copy-start
  21.2 0.0 copy-start.1
  21.3 0.0 copy-done.3
  21.3 0.0 copy-done.6
  21.3 40.4 %attend.1 = bf16[128,4096]{1,0:T(8,128)(2,1)S(1)} custom-call(s32[128]{0:T(128)S(1)} %copy-done.6, f32[8,2,128,128]{3,2,1,0:T(8,128)S(1)} %get-tuple-element.6.qh_ref, bf16[128,128,256]{2,1,0:T(8,128)(2,1)S(1)} %get-tuple-element.17.kc_ref, bf16[128,128,256]{2,1,0:T(8,128)(2,1)S(1)} %get-tuple-element.18.vc_ref, bf16[128,4096]{1,0:T(8,128)(2,1)S(1)} %copy-done.3, ...), custom_call_target="tpu_custom_call" | custom-call | flops 4294967296 | bytes 16777216 | tf_op jit(solution)/shard_map/attend/pallas_call | solution.py:348
  61.7 0.0 copy-done
  61.7 0.0 copy-done.1
  61.7 1.0 %copy.13 = bf16[128,4096]{1,0:T(8,128)(2,1)} copy(bf16[128,4096]{1,0:T(8,128)(2,1)S(1)} %attend.1) | data formatting | bytes 2097152
  (2 shorter events, 0.0 us)
Async XLA Ops:
  3.1 1.2 %copy-start.2 = (bf16[128,4096]{1,0:T(8,128)(2,1)S(1)}, bf16[128,4096]{1,0:T(8,128)(2,1)}, u32[]{:S(2)}) copy-start(bf16[128,4096]{1,0:T(8,128)(2,1)} %hid_ref.3) | copy-start | bytes 3145732
  4.3 1.6 %copy-start.4 = (bf16[4096,256]{1,0:T(8,128)(2,1)S(1)}, bf16[4096,256]{1,0:T(8,128)(2,1)}, u32[]{:S(2)}) copy-start(bf16[4096,256]{1,0:T(8,128)(2,1)} %wk_hbm.1) | copy-start | bytes 6291460
  5.9 1.6 %copy-start.5 = (bf16[4096,256]{1,0:T(8,128)(2,1)S(1)}, bf16[4096,256]{1,0:T(8,128)(2,1)}, u32[]{:S(2)}) copy-start(bf16[4096,256]{1,0:T(8,128)(2,1)} %wv_hbm.1) | copy-start | bytes 6291460
  7.5 8.4 %copy-start.7 = (bf16[128,128,256]{2,1,0:T(8,128)(2,1)S(1)}, bf16[128,128,256]{2,1,0:T(8,128)(2,1)}, u32[]{:S(2)}) copy-start(bf16[128,128,256]{2,1,0:T(8,128)(2,1)} %param.16) | copy-start | bytes 25165828
  15.9 5.4 %copy-start.3 = (bf16[128,4096]{1,0:T(8,128)(2,1)S(1)}, bf16[128,4096]{1,0:T(8,128)(2,1)}, u32[]{:S(2)}) copy-start(bf16[128,4096]{1,0:T(8,128)(2,1)} %hid_ref.3) | copy-start | bytes 3145732
  15.9 5.4 %copy-start.6 = (s32[128]{0:T(128)S(1)}, s32[128]{0:T(128)}, u32[]{:S(2)}) copy-start(s32[128]{0:T(128)} %len_ref.1) | copy-start | bytes 1540
  21.2 40.5 %copy-start = (bf16[128,128,256]{2,1,0:T(8,128)(2,1)}, bf16[128,128,256]{2,1,0:T(8,128)(2,1)S(1)}, u32[]{:S(2)}) copy-start(bf16[128,128,256]{2,1,0:T(8,128)(2,1)S(1)} %get-tuple-element.18.vc_ref) | copy-start | bytes 25165828
  21.2 40.5 %copy-start.1 = (bf16[128,128,256]{2,1,0:T(8,128)(2,1)}, bf16[128,128,256]{2,1,0:T(8,128)(2,1)S(1)}, u32[]{:S(2)}) copy-start(bf16[128,128,256]{2,1,0:T(8,128)(2,1)S(1)} %get-tuple-element.17.kc_ref) | copy-start | bytes 25165828

commit v2 on v1

--- a/solution.py
+++ b/solution.py
@@ -21,53 +21,105 @@
     return jnp.concatenate([low * cos_t - high * sin_t, high * cos_t + low * sin_t], axis=-1)
 
 
-def project_kernel(hid_ref, wn_ref, cos_ref, sin_ref, wk_hbm, wv_hbm, wq_hbm, q_ref, k_ref, v_ref,
-                   xn, wk, wv, wq, sem_k, sem_v, sem_q):
-    rows, head_dim = hid_ref.shape[0], wk.shape[1]
+def project_kernel(len_ref, hid_hbm, wn_ref, wk_hbm, wv_hbm, wq_hbm, kc_hbm, vc_hbm, q_ref, k_ref, v_ref, slot_ref,
+                   kc, vc, hid, xn, wk, wv, wq, mine, theirs, sem_h, sem_k, sem_v, sem_q, sem_c, x_s, x_r):
+    f32, bf16 = jnp.float32, jnp.bfloat16
+    rows, width = hid.shape
+    head_dim = wk.shape[1]
     heads, half = wq.shape[0], head_dim // 2
-    brows = rows // q_ref.shape[0]
-    core = lax.rem(lax.axis_index('sp'), 2)
+    brows = rows // q_ref.shape[1]
+    me = lax.axis_index('sp')
+    core = lax.rem(me, 2)
+    partner = {'sp': me + 1 - 2 * core}
 
     def q_copy(j):
         columns = pl.ds(pl.multiple_of((core * heads + j) * head_dim, head_dim), head_dim)
         return pltpu.make_async_copy(wq_hbm.at[:, columns], wq.at[j], sem_q.at[j])
 
+    crows = kc.shape[0] // heads
+
+    def cache_copies(j):
+        part = pl.ds(j * crows, crows)
+        return (pltpu.make_async_copy(kc_hbm.at[part], kc.at[part], sem_c.at[0, j]),
+                pltpu.make_async_copy(vc_hbm.at[part], vc.at[part], sem_c.at[1, j]))
+
+    def exchange(j):
+        return pltpu.make_async_remote_copy(src_ref=mine.at[j], dst_ref=theirs.at[j], send_sem=x_s.at[j],
+                                            recv_sem=x_r.at[j], device_id=partner, device_id_type=MESH)
+
+    h_copy = pltpu.make_async_copy(hid_hbm, hid, sem_h)
     k_copy = pltpu.make_async_copy(wk_hbm, wk, sem_k)
     v_copy = pltpu.make_async_copy(wv_hbm, wv, sem_v)
+    h_copy.start()
     k_copy.start()
     v_copy.start()
     for j in range(heads):
         q_copy(j).start()
-    x = hid_ref[...].astype(jnp.float32)
+    barrier = pltpu.get_barrier_semaphore()
+    pl.semaphore_signal(barrier, inc=1, device_id=partner, device_id_type=MESH)
+
+    lengths = len_ref[...].reshape(1, rows)
+    across = lax.broadcasted_iota(jnp.int32, (rows, rows), 1)
+    down = lax.broadcasted_iota(jnp.int32, (rows, rows), 0)
+    column = jnp.sum(jnp.where(across == down, lengths, 0).astype(f32), axis=1, keepdims=True)
+    slots = slot_ref.shape[1]
+    slot = lax.broadcasted_iota(jnp.int32, (rows, slots), 1) + me * slots
+    slot_ref[...] = (slot.astype(f32) == column).astype(jnp.int32)
+    angles = column * wn_ref[0:1, width:width + half]
+    cos_t, sin_t = jnp.cos(angles), jnp.sin(angles)
+
+    h_copy.wait()
+    x = hid[...].astype(f32)
     inv_rms = lax.rsqrt(jnp.mean(x * x, axis=-1, keepdims=True) + EPSILON)
-    xn[...] = (x * inv_rms * (1.0 + wn_ref[...].astype(jnp.float32))).astype(jnp.bfloat16)
-    cos_t, sin_t = cos_ref[...], sin_ref[...]
+    xn[...] = (x * inv_rms * (1.0 + wn_ref[:, 0:width])).astype(bf16)
 
     def project(w):
-        y = jnp.dot(xn[...], w, preferred_element_type=jnp.float32)
-        return y.astype(jnp.bfloat16)
+        y = jnp.dot(xn[...], w, preferred_element_type=f32)
+        return y.astype(bf16)
 
     k_copy.wait()
-    k_ref[...] = rotate(project(wk[...]).astype(jnp.float32), cos_t, sin_t).astype(jnp.bfloat16)
+    k_ref[...] = rotate(project(wk[...]).astype(f32), cos_t, sin_t).astype(bf16)
     v_copy.wait()
     v_ref[...] = project(wv[...])
+    pl.semaphore_wait(barrier, 1)
+
+    def place(k, j, y):
+        for i in range(q_ref.shape[1]):
+            for d in range(2):
+                q_ref[k, i, d, pl.ds(j, brows, stride=heads), :] = y[i * brows:(i + 1) * brows, d * half:(d + 1) * half]
 
     def one_head(j, carry):
         q_copy(j).wait()
-        y = project(wq[j]).astype(jnp.float32)
-        y = (rotate(y, cos_t, sin_t) * head_dim ** -0.5).astype(jnp.bfloat16).astype(jnp.float32)
-        for i in range(q_ref.shape[0]):
-            for d in range(2):
-                q_ref[i, d, pl.ds(j, brows, stride=heads), :] = y[i * brows:(i + 1) * brows, d * half:(d + 1) * half]
+        for copy in cache_copies(j):
+            copy.start()
+        y = project(wq[j]).astype(f32)
+        mine[j] = (rotate(y, cos_t, sin_t) * head_dim ** -0.5).astype(bf16).astype(f32)
+        exchange(j).start()
+        place(core, j, mine[j])
         return carry
 
     lax.fori_loop(0, heads, one_head, 0)
 
-
-def attend_kernel(len_ref, qh_ref, kc_ref, vc_ref, hid_ref, wo_hbm, out_ref,
-                  q_all, p_buf, num, stat_src, stat_dst, d_recv, s_sum, r_recv, l_recv, from_left, from_right,
+    def their_head(j, carry):
+        exchange(j).wait_recv()
+        place(1 - core, j, theirs[j])
+        return carry
+
+    lax.fori_loop(0, heads, their_head, 0)
+
+    def finish(j, carry):
+        exchange(j).wait_send()
+        for copy in cache_copies(j):
+            copy.wait()
+        return carry
+
+    lax.fori_loop(0, heads, finish, 0)
+
+
+def attend_kernel(len_ref, q_all, kc_ref, vc_ref, hid_ref, wo_hbm, out_ref,
+                  p_buf, num, stat_src, stat_dst, d_recv, s_sum, r_recv, l_recv, from_left, from_right,
                   att, a_bf, wo, gath, other,
-                  sem_wo, sem_ql, q_s, q_r, st_s, st_r, d_s, d_r, rs_s, rs_r, at_s, at_r,
+                  sem_wo, st_s, st_r, d_s, d_r, rs_s, rs_r, at_s, at_r,
                   own_s, own_r, fw_s, fw_r, h_s, h_r):
     f32, bf16 = jnp.float32, jnp.bfloat16
     me = lax.axis_index('sp')
@@ -96,26 +148,9 @@
         columns = pl.ds(pl.multiple_of((core * nq + j) * hd, hd), hd)
         return pltpu.make_async_copy(wo_hbm.at[:, columns], wo.at[j], sem_wo.at[j])
 
-    for j in range(nq):
-        wo_copy(j).start()
-
     barrier = pltpu.get_barrier_semaphore()
     for d in range(1, peers):
         pl.semaphore_signal(barrier, inc=1, device_id={'sp': lax.rem(me + d, peers)}, device_id_type=MESH)
-    pl.semaphore_wait(barrier, peers - 1)
-
-    nqc = q_s.shape[0]
-    per = nblk // nqc
-    q_sends, q_local = [], []
-    for t in range(nqc):
-        part = pl.ds(t * per, per)
-        copy = remote(qh_ref.at[part], q_all.at[core, part], q_s.at[t], q_r.at[t], partner)
-        copy.start()
-        q_sends.append(copy)
-        copy = pltpu.make_async_copy(qh_ref.at[part], q_all.at[core, part], sem_ql.at[t])
-        copy.start()
-        q_local.append(copy)
-
     lane = lax.broadcasted_iota(jnp.int32, (heads, slots), 1)
     position = me * slots + lane
 
@@ -139,16 +174,13 @@
         stat_src[kk] = stat
 
     stat_src[...] = jnp.zeros_like(stat_src)
-    for t in range(nqc):
-        q_local[t].wait()
-        q_sends[t].wait_recv()
-
-        def pair(u, carry):
-            i = t * per + u
-            scores(i, lax.rem(i, 2))
-            return carry
-
-        lax.fori_loop(0, per, pair, 0)
+
+    def block_scores(i, carry):
+        scores(i, lax.rem(i, 2))
+        return carry
+
+    lax.fori_loop(0, nblk, block_scores, 0)
+    pl.semaphore_wait(barrier, peers - 1)
 
     st_sends = []
     for d in range(1, peers):
@@ -175,6 +207,8 @@
         d_sends.append(copy)
         values(2 * places[t] + core)
 
+    for j in range(nq):
+        wo_copy(j).start()
     for copy in st_sends:
         copy.wait_recv()
     mine = stat_src[core]
@@ -293,7 +327,7 @@
             to_mate(which, c, n).wait_recv()
             out_ref[rows_of(c), columns_of(mate, n)] = other[c, n].astype(bf16)
 
-    for copy in q_sends + st_sends + d_sends + [r1, l1, r2a, l2a, r2b, l2b, at_copy]:
+    for copy in st_sends + d_sends + [r1, l1, r2a, l2a, r2b, l2b, at_copy]:
         copy.wait_send()
     for n in range(nq):
         for copy in own_copies(n):
@@ -312,46 +346,53 @@
     nblk = 2 * CHIPS
     brows = rows // nblk
     inv_freq = ROPE_BASE ** (-jnp.arange(hd // 2, dtype=f32) * 2.0 / hd)
-    angles = cache_len.astype(f32)[:, None] * inv_freq[None, :]
-    cos_t, sin_t = jnp.cos(angles), jnp.sin(angles)
+    gain_freq = jnp.concatenate([w_norm.astype(f32), inv_freq]).reshape(1, width + hd // 2)
     vmem = pl.BlockSpec(memory_space=pltpu.VMEM)
     hbm = pl.BlockSpec(memory_space=pl.ANY)
     smem = pl.BlockSpec(memory_space=pltpu.SMEM)
     dma = pltpu.SemaphoreType.DMA
 
-    qh, k_rot, v_new = pl.pallas_call(
+    def keep(x):
+        return pltpu.with_memory_space_constraint(x, pltpu.HBM)
+
+    def near(x):
+        return pltpu.with_memory_space_constraint(x, pltpu.VMEM)
+
+    q_all, k_rot, v_new, slot, k_near, v_near = pl.pallas_call(
         project_kernel,
-        out_shape=(jax.ShapeDtypeStruct((nblk, 2, brows * hh, hd // 2), f32), jax.ShapeDtypeStruct((rows, hd), bf16),
-                   jax.ShapeDtypeStruct((rows, hd), bf16)),
-        in_specs=[vmem] * 4 + [hbm] * 3,
-        out_specs=(vmem,) * 3,
+        out_shape=(pltpu.VMEM((2, nblk, 2, brows * hh, hd // 2), f32), jax.ShapeDtypeStruct((rows, hd), bf16),
+                   jax.ShapeDtypeStruct((rows, hd), bf16), jax.ShapeDtypeStruct((rows, seq_block), jnp.int32),
+                   pltpu.VMEM(k_block.shape, bf16), pltpu.VMEM(v_block.shape, bf16)),
+        in_specs=[vmem, hbm, vmem] + [hbm] * 5,
+        out_specs=(vmem,) * 6,
         scratch_shapes=[
+            pltpu.VMEM((rows, width), bf16),
             pltpu.VMEM((rows, width), bf16),
             pltpu.VMEM((width, hd), bf16),
             pltpu.VMEM((width, hd), bf16),
             pltpu.VMEM((hh, width, hd), bf16),
-            dma, dma, dma((hh,)),
+            pltpu.VMEM((hh, rows, hd), f32),
+            pltpu.VMEM((hh, rows, hd), f32),
+            dma, dma, dma, dma((hh,)), dma((2, hh)), dma((hh,)), dma((hh,)),
         ],
-        compiler_params=pltpu.CompilerParams(vmem_limit_bytes=28 * MIB),
+        compiler_params=pltpu.CompilerParams(collective_id=1, has_side_effects=True, vmem_limit_bytes=27 * MIB),
         cost_estimate=pl.CostEstimate(flops=2 * rows * width * (hh + 2) * hd, bytes_accessed=2 * width * (hh + 2) * hd,
                                       transcendentals=0),
         name='project',
-    )(hidden, w_norm.reshape(1, width), cos_t, sin_t, w_k, w_v, w_q)
-
-    positions = lax.axis_index('sp') * seq_block + jnp.arange(seq_block)
-    at_slot = (positions[None, :] == cache_len[:, None])[:, :, None]
-    new_k_block = jnp.where(at_slot, k_rot[:, None, :], k_block)
-    new_v_block = jnp.where(at_slot, v_new[:, None, :], v_block)
+    )(cache_len, keep(hidden), gain_freq, keep(w_k), keep(w_v), keep(w_q), keep(k_block), keep(v_block))
+
+    at_slot = (slot != 0)[:, :, None]
+    new_k_block = jnp.where(at_slot, k_rot[:, None, :], k_near)
+    new_k_block, v_near = lax.optimization_barrier((new_k_block, v_near))
+    new_v_block = jnp.where(at_slot, v_new[:, None, :], v_near)
 
     block, hl = brows * heads, hd // 2
-    nqc = CHIPS
     out_hidden = pl.pallas_call(
         attend_kernel,
         out_shape=jax.ShapeDtypeStruct((rows, width), bf16),
         in_specs=[smem, vmem, vmem, vmem, vmem, hbm],
         out_specs=vmem,
         scratch_shapes=[
-            pltpu.VMEM((2, nblk, 2, brows * hh, hl), f32),
             pltpu.VMEM((rows, heads, seq_block), bf16),
             pltpu.VMEM((nblk, 2, block, hl), f32),
             pltpu.VMEM((2, heads, seq_block), f32),
@@ -367,15 +408,15 @@
             pltpu.VMEM((hh, width, hd), bf16),
             pltpu.VMEM((CHIPS, hh, 2 * brows, hd), f32),
             pltpu.VMEM((CHIPS, hh, 2 * brows, hd), f32),
-            dma((hh,)), dma((nqc,)), dma((nqc,)), dma((nqc,)), dma((nblk - 1,)), dma((nblk - 1,)),
+            dma((hh,)), dma((nblk - 1,)), dma((nblk - 1,)),
             dma((CHIPS,)), dma((CHIPS,)), dma((6,)), dma((6,)), dma, dma,
             dma((2, hh)), dma((2, hh)), dma((hh,)), dma((hh,)), dma((CHIPS, hh)), dma((CHIPS, hh)),
         ],
-        compiler_params=pltpu.CompilerParams(collective_id=0, has_side_effects=True, vmem_limit_bytes=34 * MIB),
+        compiler_params=pltpu.CompilerParams(collective_id=0, has_side_effects=True, vmem_limit_bytes=27 * MIB),
         cost_estimate=pl.CostEstimate(flops=2 * rows * width * hh * hd * 2, bytes_accessed=2 * width * hh * hd,
                                       transcendentals=0),
         name='attend',
-    )(cache_len, qh, new_k_block, new_v_block, hidden, w_o)
+    )(cache_len, near(q_all), near(new_k_block), near(new_v_block), hidden, keep(w_o))
     return out_hidden, new_k_block, new_v_block
 
 

time: 63 us -> 61.8 us (0.981)
  local copies, waits for them, and re-layouts: 7.26 us -> 2.2 us
  Pallas kernels: 47.6 us -> 52.4 us
  other arithmetic: 7.07 us -> 6.37 us
    pallas_call x1, Pallas kernels: 7.2 us -> 15 us  [local_step(): pl.pallas_call(project_kernel, out_shape=(pltpu.VMEM((2, nblk, 2, brows *...]
    unnamed x17 -> x9, local copies, waits for them, and re-layouts: 6.55 us -> 2.19 us
    pallas_call x1, Pallas kernels: 40.4 us -> 37.4 us  [local_step(): pl.pallas_call(attend_kernel, out_shape=jax.ShapeDtypeStruct((rows, width...]
    eq x1 -> x0, other arithmetic: 0.74 us -> none  [local_step(): at_slot = (positions[None, :] == cache_len[:, None])[:, :, None]]
    reshape x1, local copies, waits for them, and re-layouts: 0.71 us -> 0.01 us  [local_step(): jnp.concatenate([w_norm.astype(f32), inv_freq]).reshape(1, width + hd // 2)]
    select_n x1 -> x2, other arithmetic: 5.35 us -> 5.64 us  [the longest x1 2.82 us: local_step(): new_k_block = jnp.where(at_slot, k_rot[:, None, :], k_near)]
where the time goes in v2:
time: 61.8 us; the launch traced here: 61.6 us
  Pallas kernels  52.4 us (85%)
  other arithmetic  6.37 us (10%)
  local copies, waits for them, and re-layouts  2.2 us (4%)
  between operations  0.71 us (1%)
    pallas_call x1, Pallas kernels, local_step(): pl.pallas_call(attend_kernel, out_shape=jax.ShapeDtypeStruct((rows, width...  37.4 us
    pallas_call x1, Pallas kernels, local_step(): pl.pallas_call(project_kernel, out_shape=(pltpu.VMEM((2, nblk, 2, brows *...  15 us
    select_n x1, other arithmetic, local_step(): new_k_block = jnp.where(at_slot, k_rot[:, None, :], k_near)  2.82 us
    select_n x1, other arithmetic, local_step(): new_v_block = jnp.where(at_slot, v_new[:, None, :], v_near)  2.82 us
    unnamed x9, local copies, waits for them, and re-layouts  2.19 us

profile of v2, /device:TPU:81, one launch (start us, length us, event | category | flops | bytes accessed | tf_op | source)
XLA Modules:
  0.0 61.6 jit_solution(5103735150853843239)
XLA Ops:
  0.6 0.7 %convert_element_type.3 = f32[4096]{0:T(1024)S(1)} convert(bf16[4096]{0:T(1024)(128)(2,1)} %param.10) | non-fusion elementwise | flops 4096 | bytes 24576 | tf_op jit(solution)/shard_map/convert_element_type | solution.py:349
  1.4 0.0 copy-start.3
  1.4 0.6 %copy-done.3 = s32[128]{0:T(128)S(1)} copy-done((s32[128]{0:T(128)S(1)}, s32[128]{0:T(128)}, u32[]{:S(2)}) %copy-start.3) | copy-done | bytes 536
  2.0 15.0 %project.1 = (f32[2,8,2,128,128]{4,3,2,1,0:T(8,128)S(1)}, bf16[128,256]{1,0:T(8,128)(2,1)S(1)}, bf16[128,256]{1,0:T(8,128)(2,1)S(1)}, s32[128,128]{1,0:T(8,128)S...) custom-call(s32[128]{0:T(128)S(1)} %copy-done.3, bf16[128,4096]{1,0:T(8,128)(2,1)} %hid_ref.1, ...), custom_call_target="tpu_custom_call" | custom-call | flops 2684354560 | bytes 20971520 | tf_op jit(solution)/shard_map/project/pallas_call | solution.py:361
  17.0 2.8 %broadcast_select_fusion.1.kc_ref = bf16[128,128,256]{2,1,0:T(8,128)(2,1)S(1)} fusion(bf16[128,128,256]{2,1,0:T(8,128)(2,1)S(1)} %get-tuple-element.14, pred[128,128]{1,0:T(8,128)(4,1)S(1)} %broadcast_compare_fusion, bf16[128,256]{1,0:T(8,128)(2,1)S(1)} %get-tuple-element.13), kind=kLoop, calls=%fused_computation.1 | loop fusion | flops 4194304 | bytes 16859136 | tf_op jit(solution)/shard_map/jit(_where)/select_n | solution.py:385
  19.9 0.0 copy-start
  19.9 0.0 copy-start.2
  19.9 2.8 %broadcast_select_fusion.vc_ref = bf16[128,128,256]{2,1,0:T(8,128)(2,1)S(1)} fusion(bf16[128,128,256]{2,1,0:T(8,128)(2,1)S(1)} %get-tuple-element.18, pred[128,128]{1,0:T(8,128)(4,1)S(1)} %broadcast_compare_fusion, bf16[128,256]{1,0:T(8,128)(2,1)S(1)} %get-tuple-element.17), kind=kLoop, calls=%fused_computation | loop fusion | flops 4194304 | bytes 16859136 | tf_op jit(solution)/shard_map/jit(_where)/select_n | solution.py:387
  22.7 0.5 copy-done
  23.3 0.0 copy-done.2
  23.3 0.0 copy-start.1
  23.3 37.4 %attend.1 = bf16[128,4096]{1,0:T(8,128)(2,1)S(1)} custom-call(s32[128]{0:T(128)S(1)} %copy-done.3, f32[2,8,2,128,128]{4,3,2,1,0:T(8,128)S(1)} %get-tuple-element.11.q_all, bf16[128,128,256]{2,1,0:T(8,128)(2,1)S(1)} %broadcast_select_fusion.1.kc_ref, bf16[128,128,256]{2,1,0:T(8,128)(2,1)S(1)} %broadcast_select_fusion.vc_ref, bf16[128,4096]{1,0:T(8,128)(2,1)S(1)} %copy-done.2, ...), custom_call_target="tpu_custom_call" | custom-call | flops 4294967296 | bytes 16777216 | tf_op jit(solution)/shard_map/attend/pallas_call | solution.py:390
  60.7 0.0 copy-done.1
  60.7 1.0 %copy.13 = bf16[128,4096]{1,0:T(8,128)(2,1)} copy(bf16[128,4096]{1,0:T(8,128)(2,1)S(1)} %attend.1) | data formatting | bytes 2097152
  (4 shorter events, 0.0 us)
Async XLA Ops:
  1.4 0.7 %copy-start.3 = (s32[128]{0:T(128)S(1)}, s32[128]{0:T(128)}, u32[]{:S(2)}) copy-start(s32[128]{0:T(128)} %len_ref.3) | copy-start | bytes 1540
  19.9 3.4 %copy-start = (bf16[128,128,256]{2,1,0:T(8,128)(2,1)}, bf16[128,128,256]{2,1,0:T(8,128)(2,1)S(1)}, u32[]{:S(2)}) copy-start(bf16[128,128,256]{2,1,0:T(8,128)(2,1)S(1)} %broadcast_select_fusion.1.kc_ref) | copy-start | bytes 25165828
  19.9 3.4 %copy-start.2 = (bf16[128,4096]{1,0:T(8,128)(2,1)S(1)}, bf16[128,4096]{1,0:T(8,128)(2,1)}, u32[]{:S(2)}) copy-start(bf16[128,4096]{1,0:T(8,128)(2,1)} %hid_ref.1) | copy-start | bytes 3145732
  23.3 37.4 %copy-start.1 = (bf16[128,128,256]{2,1,0:T(8,128)(2,1)}, bf16[128,128,256]{2,1,0:T(8,128)(2,1)S(1)}, u32[]{:S(2)}) copy-start(bf16[128,128,256]{2,1,0:T(8,128)(2,1)S(1)} %broadcast_select_fusion.vc_ref) | copy-start | bytes 25165828

commit v3 on v0

v3 whole, which is shorter than its diff:
```python
import functools

import jax
import jax.numpy as jnp
from jax import lax
from jax.experimental import pallas as pl
from jax.experimental.pallas import tpu as pltpu
from jax.sharding import PartitionSpec as P

ROPE_BASE = 10000.0
EPSILON = 1e-6
MESH = pl.DeviceIdType.MESH
MIB = 1 << 20
LOWEST = float(jnp.finfo(jnp.float32).min)
CROWS = 8
CHIPS = 4


def rotate(x, cos_t, sin_t):
    half = x.shape[-1] // 2
    low, high = x[:, :half], x[:, half:]
    return jnp.concatenate([low * cos_t - high * sin_t, high * cos_t + low * sin_t], axis=-1)


def project_kernel(len_hbm, hid_hbm, wn_hbm, fr_ref, wk_hbm, wv_hbm, wq_hbm, q_ref, k_ref, v_ref, slot_ref,
                   lens, wn, hid, xn, wkv, wq, kv, mine, theirs, sem_l, sem_n, sem_h, sem_k, sem_v, sem_q, kv_s, kv_r,
                   x_s, x_r):
    f32, bf16 = jnp.float32, jnp.bfloat16
    rows = hid.shape[0]
    head_dim = wq.shape[2]
    heads, half = wq.shape[0], head_dim // 2
    brows = rows // q_ref.shape[1]
    me = lax.axis_index('sp')
    core = lax.rem(me, 2)
    partner = {'sp': me + 1 - 2 * core}

    def q_copy(j):
        columns = pl.ds(pl.multiple_of((core * heads + j) * head_dim, head_dim), head_dim)
        return pltpu.make_async_copy(wq_hbm.at[:, columns], wq.at[j], sem_q.at[j])

    def exchange(j):
        return pltpu.make_async_remote_copy(src_ref=mine.at[j], dst_ref=theirs.at[j], send_sem=x_s.at[j],
                                            recv_sem=x_r.at[j], device_id=partner, device_id_type=MESH)

    part = pl.ds(pl.multiple_of(core * half, half), half)
    l_copy = pltpu.make_async_copy(len_hbm, lens, sem_l)
    n_copy = pltpu.make_async_copy(wn_hbm, wn, sem_n)
    h_copy = pltpu.make_async_copy(hid_hbm, hid, sem_h)
    k_copy = pltpu.make_async_copy(wk_hbm.at[:, part], wkv.at[:, pl.ds(0, half)], sem_k)
    v_copy = pltpu.make_async_copy(wv_hbm.at[:, part], wkv.at[:, pl.ds(half, half)], sem_v)
    for copy in (l_copy, n_copy, h_copy, k_copy, v_copy):
        copy.start()
    for j in range(heads):
        q_copy(j).start()
    barrier = pltpu.get_barrier_semaphore()
    pl.semaphore_signal(barrier, inc=1, device_id=partner, device_id_type=MESH)

    l_copy.wait()
    lengths = lens[...].reshape(1, rows)
    across = lax.broadcasted_iota(jnp.int32, (rows, rows), 1)
    down = lax.broadcasted_iota(jnp.int32, (rows, rows), 0)
    column = jnp.sum(jnp.where(across == down, lengths, 0).astype(f32), axis=1, keepdims=True)
    slots = slot_ref.shape[1]
    slot = lax.broadcasted_iota(jnp.int32, (rows, slots), 1) + me * slots
    slot_ref[...] = (slot.astype(f32) == column).astype(jnp.int32)
    angles = column * fr_ref[...]
    cos_t, sin_t = jnp.cos(angles), jnp.sin(angles)

    n_copy.wait()
    gain = 1.0 + wn[...].astype(f32).reshape(1, wn.shape[0])
    h_copy.wait()
    x = hid[...].astype(f32)
    inv_rms = lax.rsqrt(jnp.mean(x * x, axis=-1, keepdims=True) + EPSILON)
    xn[...] = (x * inv_rms * gain).astype(bf16)

    def project(w):
        y = jnp.dot(xn[...], w, preferred_element_type=f32)
        return y.astype(bf16)

    k_copy.wait()
    v_copy.wait()
    y = project(wkv[...]).astype(f32)
    kv[core, 0] = y[:, 0:half]
    kv[core, 1] = y[:, half:2 * half]
    pl.semaphore_wait(barrier, 1)
    kv_copy = pltpu.make_async_remote_copy(src_ref=kv.at[core], dst_ref=kv.at[core], send_sem=kv_s, recv_sem=kv_r,
                                           device_id=partner, device_id_type=MESH)
    kv_copy.start()

    def place(k, j, y):
        for i in range(q_ref.shape[1]):
            for d in range(2):
                q_ref[k, i, d, pl.ds(j, brows, stride=heads), :] = y[i * brows:(i + 1) * brows, d * half:(d + 1) * half]

    def one_head(j, carry):
        q_copy(j).wait()
        y = project(wq[j]).astype(f32)
        mine[j] = (rotate(y, cos_t, sin_t) * head_dim ** -0.5).astype(bf16).astype(f32)
        exchange(j).start()
        place(core, j, mine[j])
        return carry

    lax.fori_loop(0, heads, one_head, 0)
    kv_copy.wait_recv()
    k_ref[...] = rotate(jnp.concatenate([kv[0, 0], kv[1, 0]], axis=-1), cos_t, sin_t).astype(bf16)
    v_ref[...] = jnp.concatenate([kv[0, 1], kv[1, 1]], axis=-1).astype(bf16)

    def their_head(j, carry):
        exchange(j).wait_recv()
        place(1 - core, j, theirs[j])
        return carry

    lax.fori_loop(0, heads, their_head, 0)
    kv_copy.wait_send()

    def finish(j, carry):
        exchange(j).wait_send()
        return carry

    lax.fori_loop(0, heads, finish, 0)


def attend_kernel(len_ref, q_all, kc_ref, vc_ref, hid_ref, wo_hbm, out_ref,
                  mine, theirs, r_recv, l_recv, from_left, from_right, att, a_bf, wo, gath, other,
                  sem_wo, d_s, d_r, rs_s, rs_r, at_s, at_r, own_s, own_r, fw_s, fw_r, h_s, h_r):
    f32, bf16 = jnp.float32, jnp.bfloat16
    me = lax.axis_index('sp')
    chip, core = me // 2, lax.rem(me, 2)
    mate = 1 - core
    peers = 2 * CHIPS
    slots = kc_ref.shape[1]
    urows = 2 * CROWS
    hrows = CROWS // 2
    hl = att.shape[4]
    heads = att.shape[3] // CROWS
    hh = heads // 2
    hd = 2 * hl
    nq = wo.shape[0]
    nm = own_s.shape[2]
    per = nq // nm
    data = mine.shape[4] - 8

    def at(c, k):
        return {'sp': lax.rem(c + CHIPS, CHIPS) * 2 + k}

    right, left = at(chip + 1, core), at(chip - 1, core)
    partner = at(chip, mate)

    def remote(src, dst, ssem, rsem, dev):
        return pltpu.make_async_remote_copy(src_ref=src, dst_ref=dst, send_sem=ssem, recv_sem=rsem,
                                            device_id=dev, device_id_type=MESH)

    def wo_copy(j):
        columns = pl.ds(pl.multiple_of((core * nq + j) * hd, hd), hd)
        return pltpu.make_async_copy(wo_hbm.at[:, columns], wo.at[j], sem_wo.at[j])

    for j in range(nq):
        wo_copy(j).start()

    barrier = pltpu.get_barrier_semaphore()
    for dev in (right, left, partner):
        pl.semaphore_signal(barrier, inc=1, device_id=dev, device_id_type=MESH)

    lane = lax.broadcasted_iota(jnp.int32, (heads, slots), 1)
    lane8 = lax.broadcasted_iota(jnp.int32, (8, 128), 1)
    is_max = lane8 < 64
    position = me * slots + lane

    def place_of(t):
        return lax.rem(chip + 2 - t + 3 * (t // 2) - 2 * (t // 3), CHIPS)

    def attention(ph, t):
        i = 2 * place_of(t) + ph
        for kk in range(2):
            for half in range(2):
                stat = jnp.zeros((8, 128), f32)
                for r4 in range(hrows):
                    r = kk * CROWS + half * hrows + r4
                    b = i * urows + r
                    own_rows = slice(r * hh, (r + 1) * hh)
                    q = jnp.concatenate([
                        jnp.concatenate([q_all[k, i, d, own_rows, :] for k in range(2)], axis=0) for d in range(2)], axis=1)
                    s = lax.dot_general(q.astype(bf16), kc_ref[b], (((1,), (1,)), ((), ())), preferred_element_type=f32)
                    valid = position <= len_ref[b]
                    s = jnp.where(valid, s, LOWEST)
                    m = jnp.max(s, axis=1, keepdims=True)
                    p = jnp.where(valid, jnp.exp(s - m), 0.0)
                    den = jnp.sum(p, axis=1, keepdims=True)
                    o = jnp.dot(p.astype(bf16), vc_ref[b], preferred_element_type=f32)
                    for d in range(2):
                        rows = slice((d * hrows + r4) * heads, (d * hrows + r4 + 1) * heads)
                        mine[ph, t, kk, half, rows, :] = o[:, d * hl:(d + 1) * hl]
                    for g in range(2):
                        stat = jnp.where(lane8 == g * 32 + r4, m[g * 8:(g + 1) * 8],
                                         jnp.where(lane8 == 64 + g * 32 + r4, den[g * 8:(g + 1) * 8], stat))
                mine[ph, t, kk, half, data:data + 8, :] = stat

    def d_copy(ph, t):
        return remote(mine.at[ph, t, mate], theirs.at[ph, t], d_s.at[ph, t], d_r.at[ph, t], partner)

    def tiles():
        for r4 in range(hrows):
            for g in range(2):
                for d in range(2):
                    yield g * 32 + r4, (d * hrows + r4) * heads + g * 8, d, r4, g

    def merge(into, src):
        one, two = into[data:data + 8, :], src[data:data + 8, :]
        top = jnp.maximum(one, two)
        a, b = jnp.exp(one - top), jnp.exp(two - top)
        den = pltpu.roll(a, 64, 1) * one + pltpu.roll(b, 64, 1) * two
        for column, row, _, _, _ in tiles():
            into[row:row + 8, :] = (into[row:row + 8, :] * a[:, column:column + 1]
                                    + src[row:row + 8, :] * b[:, column:column + 1])
        into[data:data + 8, :] = jnp.where(is_max, top, den)

    def combine(ph, t):
        d_copy(ph, t).wait_recv()
        for half in range(2):
            merge(mine.at[ph, t, core, half], theirs.at[ph, t, half])

    def ring(ph, n, src, dst, dev):
        return remote(src, dst, rs_s.at[ph, n], rs_r.at[ph, n], dev)

    def piece(ph, t, half):
        return mine.at[ph, t, core, half]

    def r1(ph):
        return ring(ph, 0, piece(ph, 0, 0), r_recv.at[ph], right)

    def l1(ph):
        return ring(ph, 1, piece(ph, 0, 1), l_recv.at[ph], left)

    def r2(ph, half):
        return ring(ph, 2 + half, piece(ph, 1, half), from_left.at[ph, half], right)

    def l2(ph, half):
        return ring(ph, 4 + half, piece(ph, 2, half), from_right.at[ph, half], left)

    def reduce_start(ph):
        combine(ph, 0)
        r1(ph).start()
        l1(ph).start()
        combine(ph, 1)
        r2(ph, 1).start()
        combine(ph, 2)
        l2(ph, 0).start()

    def reduce_turn(ph):
        r1(ph).wait_recv()
        merge(piece(ph, 1, 0), r_recv.at[ph])
        r2(ph, 0).start()
        l1(ph).wait_recv()
        merge(piece(ph, 2, 1), l_recv.at[ph])
        l2(ph, 1).start()

    def at_copy(ph):
        return remote(att.at[ph, core], att.at[ph, core], at_s.at[ph], at_r.at[ph], partner)

    def reduce_end(ph):
        for half in range(2):
            r2(ph, half).wait_recv()
            l2(ph, half).wait_recv()
            parts = [mine.at[ph, 3, core, half], from_left.at[ph, half], from_right.at[ph, half]]
            stats = [x[data:data + 8, :] for x in parts]
            top = jnp.maximum(jnp.maximum(stats[0], stats[1]), stats[2])
            scale = [jnp.exp(x - top) for x in stats]
            den = sum(a * pltpu.roll(x, 64, 1) for a, x in zip(scale, stats))
            den = jnp.where(is_max & (lane8 % 32 < hrows), den, 1.0)
            scale = [a / den for a in scale]
            for column, row, d, r4, g in tiles():
                y = sum(x[row:row + 8, :] * a[:, column:column + 1] for x, a in zip(parts, scale))
                to = (half * hrows + r4) * heads + g * 8
                att[ph, core, d, to:to + 8, :] = y
        at_copy(ph).start()

    def rows_of(c, ph):
        return pl.ds(pl.multiple_of((2 * c + ph) * urows, urows), urows)

    def columns_of(k, n):
        return pl.ds(pl.multiple_of((k * nq + n) * hd, hd), hd)

    def own_copies(ph, u):
        src = gath.at[ph, chip, pl.ds(u * per, per)]
        return (remote(src, src, own_s.at[ph, 0, u], own_r.at[ph, 0, u], right),
                remote(src, src, own_s.at[ph, 1, u], own_r.at[ph, 1, u], left),
                to_mate(ph, 0, chip, u))

    def to_mate(ph, which, c, u):
        part = pl.ds(u * per, per)
        return remote(gath.at[ph, c, part], other.at[ph, c, part], h_s.at[ph, which, u], h_r.at[ph, which, u], partner)

    def project(ph, first):
        at_copy(ph).wait_recv()
        for h in range(heads):
            for d in range(2):
                pair = [att[ph, kk, d, pl.ds(h, CROWS, stride=heads), :] for kk in range(2)]
                a_bf[ph, :, h * hd + d * hl:h * hd + (d + 1) * hl] = jnp.concatenate(pair, axis=0).astype(bf16)

        def message(u, carry):
            for v in range(per):
                n = u * per + v
                if first:
                    wo_copy(n).wait()
                y = jnp.dot(a_bf[ph], wo[n], preferred_element_type=f32)
                gath[ph, chip, n] = hid_ref[rows_of(chip, ph), columns_of(core, n)].astype(f32) + y
            for copy in own_copies(ph, u):
                copy.start()
            return carry

        lax.fori_loop(0, nm, message, 0)

    cl, cr, co = place_of(2), place_of(1), place_of(0)
    split = nm // 2

    def forward(ph, u):
        c, dev = (cl, right) if u < split else (cr, left)
        src = gath.at[ph, c, pl.ds(u * per, per)]
        return remote(src, src, fw_s.at[ph, u], fw_r.at[ph, u], dev)

    def put(ph, c, u):
        for n in range(u * per, (u + 1) * per):
            out_ref[rows_of(c, ph), columns_of(core, n)] = gath[ph, c, n].astype(bf16)

    def put_other(ph, c, u):
        for n in range(u * per, (u + 1) * per):
            out_ref[rows_of(c, ph), columns_of(mate, n)] = other[ph, c, n].astype(bf16)

    def relay(ph):
        for u in range(nm):
            own_copies(ph, u)[0].wait_recv()
            if u < split:
                forward(ph, u).start()
            to_mate(ph, 1, cl, u).start()
            own_copies(ph, u)[1].wait_recv()
            if u >= split:
                forward(ph, u).start()
            to_mate(ph, 2, cr, u).start()

    def relay_end(ph):
        for u in range(nm):
            forward(ph, u).wait_recv()
            to_mate(ph, 3, co, u).start()

    places = ((0, chip), (1, cl), (2, cr), (3, co))

    def finish(ph):
        for which, c in places:
            for u in range(nm):
                put(ph, c, u)
                to_mate(ph, which, c, u).wait_recv()
                put_other(ph, c, u)

    def unit(ph):
        def body(t, carry):
            attention(ph, t)
            d_copy(ph, t).start()
            return carry

        return body

    attention(0, 0)
    pl.semaphore_wait(barrier, 3)
    d_copy(0, 0).start()
    lax.fori_loop(1, CHIPS, unit(0), 0)
    reduce_start(0)
    lax.fori_loop(0, CHIPS, unit(1), 0)
    reduce_turn(0)
    reduce_start(1)
    combine(0, 3)
    reduce_turn(1)
    combine(1, 3)
    reduce_end(0)
    project(0, True)
    reduce_end(1)
    project(1, False)
    relay(0)
    relay_end(0)
    relay(1)
    finish(0)
    relay_end(1)
    finish(1)

    for ph in range(2):
        for t in range(CHIPS):
            d_copy(ph, t).wait_send()
        for copy in (r1(ph), l1(ph), r2(ph, 0), r2(ph, 1), l2(ph, 0), l2(ph, 1), at_copy(ph)):
            copy.wait_send()
        for u in range(nm):
            for copy in own_copies(ph, u):
                copy.wait_send()
            forward(ph, u).wait_send()
            for which, c in places[1:]:
                to_mate(ph, which, c, u).wait_send()


def local_step(hidden, w_norm, w_q, w_k, w_v, w_o, k_block, v_block, cache_len):
    f32, bf16 = jnp.float32, jnp.bfloat16
    rows, width = hidden.shape
    seq_block, hd = k_block.shape[1], k_block.shape[2]
    heads = w_q.shape[1] // hd
    hh, hl = heads // 2, hd // 2
    nblk = 2 * CHIPS
    brows = rows // nblk
    assert brows == 2 * CROWS
    inv_freq = (ROPE_BASE ** (-jnp.arange(hl, dtype=f32) * 2.0 / hd)).reshape(1, hl)
    vmem = pl.BlockSpec(memory_space=pltpu.VMEM)
    hbm = pl.BlockSpec(memory_space=pl.ANY)
    smem = pl.BlockSpec(memory_space=pltpu.SMEM)
    dma = pltpu.SemaphoreType.DMA

    def keep(x):
        return pltpu.with_memory_space_constraint(x, pltpu.HBM)

    def near(x):
        return pltpu.with_memory_space_constraint(x, pltpu.VMEM)

    q_all, k_rot, v_new, slot = pl.pallas_call(
        project_kernel,
        out_shape=(pltpu.VMEM((2, nblk, 2, brows * hh, hl), f32), jax.ShapeDtypeStruct((rows, hd), bf16),
                   jax.ShapeDtypeStruct((rows, hd), bf16), jax.ShapeDtypeStruct((rows, seq_block), jnp.int32)),
        in_specs=[hbm] * 3 + [vmem] + [hbm] * 3,
        out_specs=(vmem,) * 4,
        scratch_shapes=[
            pltpu.VMEM((rows,), jnp.int32),
            pltpu.VMEM((width,), bf16),
            pltpu.VMEM((rows, width), bf16),
            pltpu.VMEM((rows, width), bf16),
            pltpu.VMEM((width, hd), bf16),
            pltpu.VMEM((hh, width, hd), bf16),
            pltpu.VMEM((2, 2, rows, hl), f32),
            pltpu.VMEM((hh, rows, hd), f32),
            pltpu.VMEM((hh, rows, hd), f32),
            dma, dma, dma, dma, dma, dma((hh,)), dma, dma, dma((hh,)), dma((hh,)),
        ],
        compiler_params=pltpu.CompilerParams(collective_id=1, has_side_effects=True, vmem_limit_bytes=56 * MIB),
        cost_estimate=pl.CostEstimate(flops=2 * rows * width * (hh + 1) * hd, bytes_accessed=2 * width * (hh + 1) * hd,
                                      transcendentals=0),
        name='project',
    )(keep(cache_len), keep(hidden), keep(w_norm), inv_freq, keep(w_k), keep(w_v), keep(w_q))

    at_slot = (slot != 0)[:, :, None]
    new_k_block = jnp.where(at_slot, k_rot[:, None, :], k_block)
    new_v_block = jnp.where(at_slot, v_new[:, None, :], v_block)

    half_rows = CROWS * heads + 8
    nm = hh // 2
    out_hidden = pl.pallas_call(
        attend_kernel,
        out_shape=jax.ShapeDtypeStruct((rows, width), bf16),
        in_specs=[smem, vmem, vmem, vmem, vmem, hbm],
        out_specs=vmem,
        scratch_shapes=[
            pltpu.VMEM((2, CHIPS, 2, 2, half_rows, hl), f32),
            pltpu.VMEM((2, CHIPS, 2, half_rows, hl), f32),
            pltpu.VMEM((2, half_rows, hl), f32),
            pltpu.VMEM((2, half_rows, hl), f32),
            pltpu.VMEM((2, 2, half_rows, hl), f32),
            pltpu.VMEM((2, 2, half_rows, hl), f32),
            pltpu.VMEM((2, 2, 2, CROWS * heads, hl), f32),
            pltpu.VMEM((2, brows, width), bf16),
            pltpu.VMEM((hh, width, hd), bf16),
            pltpu.VMEM((2, CHIPS, hh, brows, hd), f32),
            pltpu.VMEM((2, CHIPS, hh, brows, hd), f32),
            dma((hh,)), dma((2, CHIPS)), dma((2, CHIPS)), dma((2, 6)), dma((2, 6)), dma((2,)), dma((2,)),
            dma((2, 2, nm)), dma((2, 2, nm)), dma((2, nm)), dma((2, nm)), dma((2, CHIPS, nm)), dma((2, CHIPS, nm)),
        ],
        compiler_params=pltpu.CompilerParams(collective_id=0, has_side_effects=True, vmem_limit_bytes=26 * MIB),
        cost_estimate=pl.CostEstimate(flops=2 * rows * width * hh * hd * 2, bytes_accessed=2 * width * hh * hd,
                                      transcendentals=0),
        name='attend',
    )(cache_len, near(q_all), near(new_k_block), near(new_v_block), hidden, keep(w_o))
    return out_hidden, new_k_block, new_v_block


def solution(mesh):
    assert mesh.shape['sp'] == 2 * CHIPS
    cache_spec = P('dp', 'sp', None)
    return jax.shard_map(local_step, mesh=mesh, in_specs=(P('dp', None), P(None), P(None, None), P(None, None), P(None, None), P(None, None), cache_spec, cache_spec, P('dp')), out_specs=(P('dp', None), cache_spec, cache_spec), check_vma=False)
```

time: 157 us -> 87.6 us (0.56)
  Pallas kernels: 0 us -> 77.1 us
  blocking collectives: 49.8 us -> 0 us
  matrix products: 37.7 us -> 0 us
  waiting for transfers between devices: 35.3 us -> 0 us
  between operations: 14.2 us -> 0.72 us
  other arithmetic: 17 us -> 8.56 us
    pallas_call x0 -> x2, Pallas kernels: none -> 77.1 us  [the longest x1 61.4 us: local_step(): pl.pallas_call(attend_kernel, out_shape=jax.ShapeDtypeStruct((rows, width...]
    dot_general x6 -> x0, matrix products: 37.7 us -> none  [the longest x1 14.2 us: local_step(): jnp.dot(attended, w_o, preferred_element_type=jnp.float32)]
    psum x1 -> x0, waiting for transfers between devices: 35.2 us -> none  [local_step(): numerator, denominator = lax.psum((part_num, part_den), 'sp')]
    psum x1 -> x0, blocking collectives: 25.4 us -> none  [local_step(): numerator, denominator = lax.psum((part_num, part_den), 'sp')]
    pmax x1 -> x0, blocking collectives: 24.4 us -> none  [local_step(): row_max = lax.pmax(jnp.max(masked, axis=-1), 'sp')]
    convert_element_type x2 -> x0, other arithmetic: 2.72 us -> none  [the longest x1 1.93 us: local_step(): (numerator / denominator[:, :, None]).astype(jnp.bfloat16)]
    select_n x1, other arithmetic: 9.75 us -> 7.18 us  [local_step(): new_v_block = jnp.where(at_slot, v_new[:, None, :], v_block)]
    reduce_sum x2 -> x0, other arithmetic: 2.18 us -> none  [the longest x1 1.52 us: project_token(): jnp.mean(x_f32 * x_f32, axis=-1, keepdims=True) + EPSILON]
  transfers between devices with their start and end apart: 1 -> 0, of which waited for: 1 -> 0; matrix products, arithmetic and copies ran while one was open for 0% -> 0% of each run, Pallas kernels for 0% -> 0%
where the time goes in v3:
time: 87.6 us; the launch traced here: 87.4 us
  Pallas kernels  77.1 us (88%)
  other arithmetic  8.56 us (10%)
  local copies, waits for them, and re-layouts  1 us (1%)
    pallas_call x1, Pallas kernels, local_step(): pl.pallas_call(attend_kernel, out_shape=jax.ShapeDtypeStruct((rows, width...  61.4 us
    pallas_call x1, Pallas kernels, local_step(): pl.pallas_call(project_kernel, out_shape=(pltpu.VMEM((2, nblk, 2, brows *...  15.8 us
    select_n x1, other arithmetic, local_step(): new_v_block = jnp.where(at_slot, v_new[:, None, :], v_block)  7.18 us

profile of v3, /device:TPU:81, one launch (start us, length us, event | category | flops | bytes accessed | tf_op | source)
XLA Modules:
  0.0 87.4 jit_solution(16118222479670115586)
XLA Ops:
  0.6 0.5 multiply_power_fusion.fr_ref
  1.2 15.8 %project.1 = (f32[2,8,2,128,128]{4,3,2,1,0:T(8,128)S(1)}, bf16[128,256]{1,0:T(8,128)(2,1)}, bf16[128,256]{1,0:T(8,128)(2,1)}, s32[128,128]{1,0:T(8,128)}) custom-call(s32[128]{0:T(128)} %len_ref.1, bf16[128,4096]{1,0:T(8,128)(2,1)} %hid_ref.1, bf16[4096]{0:T(1024)(128)(2,1)} %wn_hbm.1, f32[1,128]{1,0:T(1,128)} %multiply_power_fusion.fr_ref, ...), custom_call_target="tpu_custom_call" | custom-call | flops 2415919104 | bytes 18874368 | tf_op jit(solution)/shard_map/project/pallas_call | solution.py:418
  16.9 0.9 broadcast_compare_fusion
  17.8 0.0 copy-start.2
  17.8 0.0 copy-start.3
  17.8 7.2 %broadcast_select_fusion = (bf16[128,128,256]{2,1,0:T(8,128)(2,1)S(1)}, bf16[128,128,256]{2,1,0:T(8,128)(2,1)S(1)}) fusion(bf16[128,128,256]{2,1,0:T(8,128)(2,1)} %param.16, pred[128,128]{1,0:T(8,128)(4,1)S(1)} %broadcast_compare_fusion, bf16[128,256]{1,0:T(8,128)(2,1)} %get-tuple-element.10, bf16[128,128,256]{2,1,0:T(8,128)(2,1)} %param.15, ...), kind=kLoop, calls=%fused_computation | loop fusion | flops 8388608 | bytes 33701888 | tf_op jit(solution)/shard_map/jit(_where)/select_n | solution.py:444
  25.0 0.0 copy-start
  25.0 0.0 copy-start.1
  25.0 0.0 copy-done.2
  25.0 0.0 copy-done.3
  25.0 61.4 %attend.1 = bf16[128,4096]{1,0:T(8,128)(2,1)S(1)} custom-call(s32[128]{0:T(128)S(1)} %copy-done.3, f32[2,8,2,128,128]{4,3,2,1,0:T(8,128)S(1)} %get-tuple-element.7.q_all, bf16[128,128,256]{2,1,0:T(8,128)(2,1)S(1)} %get-tuple-element.17.kc_ref, bf16[128,128,256]{2,1,0:T(8,128)(2,1)S(1)} %get-tuple-element.18.vc_ref, bf16[128,4096]{1,0:T(8,128)(2,1)S(1)} %copy-done.2, ...), custom_call_target="tpu_custom_call" | custom-call | flops 4294967296 | bytes 16777216 | tf_op jit(solution)/shard_map/attend/pallas_call | solution.py:448
  86.4 0.0 copy-done
  86.4 0.0 copy-done.1
  86.4 1.0 %copy.13 = bf16[128,4096]{1,0:T(8,128)(2,1)} copy(bf16[128,4096]{1,0:T(8,128)(2,1)S(1)} %attend.1) | data formatting | bytes 2097152
Async XLA Ops:
  17.8 7.2 %copy-start.2 = (bf16[128,4096]{1,0:T(8,128)(2,1)S(1)}, bf16[128,4096]{1,0:T(8,128)(2,1)}, u32[]{:S(2)}) copy-start(bf16[128,4096]{1,0:T(8,128)(2,1)} %hid_ref.1) | copy-start | bytes 3145732
  17.8 7.2 %copy-start.3 = (s32[128]{0:T(128)S(1)}, s32[128]{0:T(128)}, u32[]{:S(2)}) copy-start(s32[128]{0:T(128)} %len_ref.1) | copy-start | bytes 1540
  25.0 61.4 %copy-start = (bf16[128,128,256]{2,1,0:T(8,128)(2,1)}, bf16[128,128,256]{2,1,0:T(8,128)(2,1)S(1)}, u32[]{:S(2)}) copy-start(bf16[128,128,256]{2,1,0:T(8,128)(2,1)S(1)} %get-tuple-element.18.vc_ref) | copy-start | bytes 25165828
  25.0 61.4 %copy-start.1 = (bf16[128,128,256]{2,1,0:T(8,128)(2,1)}, bf16[128,128,256]{2,1,0:T(8,128)(2,1)S(1)}, u32[]{:S(2)}) copy-start(bf16[128,128,256]{2,1,0:T(8,128)(2,1)S(1)} %get-tuple-element.17.kc_ref) | copy-start | bytes 25165828

commit v4 on v3

--- a/solution.py
+++ b/solution.py
@@ -22,7 +22,7 @@
     return jnp.concatenate([low * cos_t - high * sin_t, high * cos_t + low * sin_t], axis=-1)
 
 
-def project_kernel(len_hbm, hid_hbm, wn_hbm, fr_ref, wk_hbm, wv_hbm, wq_hbm, q_ref, k_ref, v_ref, slot_ref,
+def project_kernel(slots, len_hbm, hid_hbm, wn_hbm, fr_ref, wk_hbm, wv_hbm, wq_hbm, q_ref, k_ref, v_ref, slot_ref,
                    lens, wn, hid, xn, wkv, wq, kv, mine, theirs, sem_l, sem_n, sem_h, sem_k, sem_v, sem_q, kv_s, kv_r,
                    x_s, x_r):
     f32, bf16 = jnp.float32, jnp.bfloat16
@@ -50,7 +50,8 @@
     v_copy = pltpu.make_async_copy(wv_hbm.at[:, part], wkv.at[:, pl.ds(half, half)], sem_v)
     for copy in (l_copy, n_copy, h_copy, k_copy, v_copy):
         copy.start()
-    for j in range(heads):
+    ahead = 3
+    for j in range(ahead):
         q_copy(j).start()
     barrier = pltpu.get_barrier_semaphore()
     pl.semaphore_signal(barrier, inc=1, device_id=partner, device_id_type=MESH)
@@ -60,9 +61,8 @@
     across = lax.broadcasted_iota(jnp.int32, (rows, rows), 1)
     down = lax.broadcasted_iota(jnp.int32, (rows, rows), 0)
     column = jnp.sum(jnp.where(across == down, lengths, 0).astype(f32), axis=1, keepdims=True)
-    slots = slot_ref.shape[1]
-    slot = lax.broadcasted_iota(jnp.int32, (rows, slots), 1) + me * slots
-    slot_ref[...] = (slot.astype(f32) == column).astype(jnp.int32)
+    first = (me * slots).astype(f32)
+    slot_ref[...] = jnp.broadcast_to((column - first).astype(jnp.int32), slot_ref.shape)
     angles = column * fr_ref[...]
     cos_t, sin_t = jnp.cos(angles), jnp.sin(angles)
 
@@ -94,6 +94,11 @@
 
     def one_head(j, carry):
         q_copy(j).wait()
+
+        @pl.when(j + ahead < heads)
+        def _():
+            q_copy(j + ahead).start()
+
         y = project(wq[j]).astype(f32)
         mine[j] = (rotate(y, cos_t, sin_t) * head_dim ** -0.5).astype(bf16).astype(f32)
         exchange(j).start()
@@ -121,7 +126,7 @@
 
 
 def attend_kernel(len_ref, q_all, kc_ref, vc_ref, hid_ref, wo_hbm, out_ref,
-                  mine, theirs, r_recv, l_recv, from_left, from_right, att, a_bf, wo, gath, other,
+                  p_buf, mine, theirs, r_recv, l_recv, from_left, from_right, att, a_bf, wo, gath, other,
                   sem_wo, d_s, d_r, rs_s, rs_r, at_s, at_r, own_s, own_r, fw_s, fw_r, h_s, h_r):
     f32, bf16 = jnp.float32, jnp.bfloat16
     me = lax.axis_index('sp')
@@ -169,7 +174,7 @@
     def place_of(t):
         return lax.rem(chip + 2 - t + 3 * (t // 2) - 2 * (t // 3), CHIPS)
 
-    def attention(ph, t):
+    def scores(ph, t):
         i = 2 * place_of(t) + ph
         for kk in range(2):
             for half in range(2):
@@ -186,14 +191,22 @@
                     m = jnp.max(s, axis=1, keepdims=True)
                     p = jnp.where(valid, jnp.exp(s - m), 0.0)
                     den = jnp.sum(p, axis=1, keepdims=True)
-                    o = jnp.dot(p.astype(bf16), vc_ref[b], preferred_element_type=f32)
-                    for d in range(2):
-                        rows = slice((d * hrows + r4) * heads, (d * hrows + r4 + 1) * heads)
-                        mine[ph, t, kk, half, rows, :] = o[:, d * hl:(d + 1) * hl]
+                    p_buf[t, r] = p.astype(bf16)
                     for g in range(2):
                         stat = jnp.where(lane8 == g * 32 + r4, m[g * 8:(g + 1) * 8],
                                          jnp.where(lane8 == 64 + g * 32 + r4, den[g * 8:(g + 1) * 8], stat))
                 mine[ph, t, kk, half, data:data + 8, :] = stat
+
+    def values(ph, t):
+        i = 2 * place_of(t) + ph
+        for kk in range(2):
+            for half in range(2):
+                for r4 in range(hrows):
+                    r = kk * CROWS + half * hrows + r4
+                    o = jnp.dot(p_buf[t, r], vc_ref[i * urows + r], preferred_element_type=f32)
+                    for d in range(2):
+                        rows = slice((d * hrows + r4) * heads, (d * hrows + r4 + 1) * heads)
+                        mine[ph, t, kk, half, rows, :] = o[:, d * hl:(d + 1) * hl]
 
     def d_copy(ph, t):
         return remote(mine.at[ph, t, mate], theirs.at[ph, t], d_s.at[ph, t], d_r.at[ph, t], partner)
@@ -351,20 +364,27 @@
                 to_mate(ph, which, c, u).wait_recv()
                 put_other(ph, c, u)
 
-    def unit(ph):
+    def scores_of(ph):
         def body(t, carry):
-            attention(ph, t)
+            scores(ph, t)
+            return carry
+
+        lax.fori_loop(0, CHIPS, body, 0)
+
+    def values_of(ph):
+        def body(t, carry):
+            values(ph, t)
             d_copy(ph, t).start()
             return carry
 
-        return body
-
-    attention(0, 0)
+        lax.fori_loop(0, CHIPS, body, 0)
+
+    scores_of(0)
     pl.semaphore_wait(barrier, 3)
-    d_copy(0, 0).start()
-    lax.fori_loop(1, CHIPS, unit(0), 0)
+    values_of(0)
+    scores_of(1)
     reduce_start(0)
-    lax.fori_loop(0, CHIPS, unit(1), 0)
+    values_of(1)
     reduce_turn(0)
     reduce_start(1)
     combine(0, 3)
@@ -416,9 +436,9 @@
         return pltpu.with_memory_space_constraint(x, pltpu.VMEM)
 
     q_all, k_rot, v_new, slot = pl.pallas_call(
-        project_kernel,
+        functools.partial(project_kernel, seq_block),
         out_shape=(pltpu.VMEM((2, nblk, 2, brows * hh, hl), f32), jax.ShapeDtypeStruct((rows, hd), bf16),
-                   jax.ShapeDtypeStruct((rows, hd), bf16), jax.ShapeDtypeStruct((rows, seq_block), jnp.int32)),
+                   jax.ShapeDtypeStruct((rows, hd), bf16), jax.ShapeDtypeStruct((rows, hd), jnp.int32)),
         in_specs=[hbm] * 3 + [vmem] + [hbm] * 3,
         out_specs=(vmem,) * 4,
         scratch_shapes=[
@@ -439,7 +459,7 @@
         name='project',
     )(keep(cache_len), keep(hidden), keep(w_norm), inv_freq, keep(w_k), keep(w_v), keep(w_q))
 
-    at_slot = (slot != 0)[:, :, None]
+    at_slot = lax.broadcasted_iota(jnp.int32, k_block.shape, 1) == slot[:, None, :]
     new_k_block = jnp.where(at_slot, k_rot[:, None, :], k_block)
     new_v_block = jnp.where(at_slot, v_new[:, None, :], v_block)
 
@@ -451,6 +471,7 @@
         in_specs=[smem, vmem, vmem, vmem, vmem, hbm],
         out_specs=vmem,
         scratch_shapes=[
+            pltpu.VMEM((CHIPS, brows, heads, seq_block), bf16),
             pltpu.VMEM((2, CHIPS, 2, 2, half_rows, hl), f32),
             pltpu.VMEM((2, CHIPS, 2, half_rows, hl), f32),
             pltpu.VMEM((2, half_rows, hl), f32),

time: 87.6 us -> 64.7 us (0.74)
  Pallas kernels: 77.1 us -> 52.4 us
  other arithmetic: 8.56 us -> 10.5 us
    pallas_call x1, Pallas kernels: 61.4 us -> 39 us  [local_step(): pl.pallas_call(attend_kernel, out_shape=jax.ShapeDtypeStruct((rows, width...]
    select_n x1, other arithmetic: 7.18 us -> 9.94 us  [local_step(): new_v_block = jnp.where(at_slot, v_new[:, None, :], v_block)]
    pallas_call x1, Pallas kernels: 15.8 us -> 13.3 us  [local_step(): pl.pallas_call(functools.partial(project_kernel, seq_block), out_shape=(p...]
where the time goes in v4:
time: 64.7 us; the launch traced here: 64.6 us
  Pallas kernels  52.4 us (81%)
  other arithmetic  10.5 us (16%)
  local copies, waits for them, and re-layouts  1 us (2%)
  between operations  0.72 us (1%)
    pallas_call x1, Pallas kernels, local_step(): pl.pallas_call(attend_kernel, out_shape=jax.ShapeDtypeStruct((rows, width...  39 us
    pallas_call x1, Pallas kernels, local_step(): pl.pallas_call(functools.partial(project_kernel, seq_block), out_shape=(p...  13.3 us
    select_n x1, other arithmetic, local_step(): new_v_block = jnp.where(at_slot, v_new[:, None, :], v_block)  9.94 us

profile of v4, /device:TPU:81, one launch (start us, length us, event | category | flops | bytes accessed | tf_op | source)
XLA Modules:
  0.0 64.6 jit_solution(13415287610760643521)
XLA Ops:
  0.6 0.5 multiply_power_fusion.fr_ref
  1.2 13.3 %project.1 = (f32[2,8,2,128,128]{4,3,2,1,0:T(8,128)S(1)}, bf16[128,256]{1,0:T(8,128)(2,1)}, bf16[128,256]{1,0:T(8,128)(2,1)}, s32[128,256]{1,0:T(8,128)}) custom-call(s32[128]{0:T(128)} %len_ref.1, bf16[128,4096]{1,0:T(8,128)(2,1)} %hid_ref.1, bf16[4096]{0:T(1024)(128)(2,1)} %wn_hbm.1, f32[1,128]{1,0:T(1,128)} %multiply_power_fusion.fr_ref, ...), custom_call_target="tpu_custom_call" | custom-call | flops 2415919104 | bytes 18874368 | tf_op jit(solution)/shard_map/project/pallas_call | solution.py:438
  14.5 0.0 copy-start.2
  14.5 0.0 copy-start.3
  14.5 9.9 %fusion = (bf16[128,128,256]{2,1,0:T(8,128)(2,1)S(1)}, bf16[128,128,256]{2,1,0:T(8,128)(2,1)S(1)}) fusion(bf16[128,128,256]{2,1,0:T(8,128)(2,1)} %param.16, s32[128,256]{1,0:T(8,128)} %get-tuple-element.8, bf16[128,256]{1,0:T(8,128)(2,1)} %get-tuple-element.10, bf16[128,128,256]{2,1,0:T(8,128)(2,1)} %param.15, bf16[128,256]{1,0:T(8,128)(2,1)} %get-tuple-element.9), kind=kLoop, calls=%fused_computation.1 | loop fusion | flops 12582912 | bytes 33816576 | tf_op jit(solution)/shard_map/jit(_where)/select_n | solution.py:464
  24.5 0.0 copy-start
  24.5 0.0 copy-start.1
  24.5 0.0 copy-done.2
  24.5 0.0 copy-done.3
  24.5 39.0 %attend.1 = bf16[128,4096]{1,0:T(8,128)(2,1)S(1)} custom-call(s32[128]{0:T(128)S(1)} %copy-done.3, f32[2,8,2,128,128]{4,3,2,1,0:T(8,128)S(1)} %get-tuple-element.7.q_all, bf16[128,128,256]{2,1,0:T(8,128)(2,1)S(1)} %get-tuple-element.17.kc_ref, bf16[128,128,256]{2,1,0:T(8,128)(2,1)S(1)} %get-tuple-element.18.vc_ref, bf16[128,4096]{1,0:T(8,128)(2,1)S(1)} %copy-done.2, ...), custom_call_target="tpu_custom_call" | custom-call | flops 4294967296 | bytes 16777216 | tf_op jit(solution)/shard_map/attend/pallas_call | solution.py:468
  63.6 0.0 copy-done
  63.6 0.0 copy-done.1
  63.6 1.0 %copy.13 = bf16[128,4096]{1,0:T(8,128)(2,1)} copy(bf16[128,4096]{1,0:T(8,128)(2,1)S(1)} %attend.1) | data formatting | bytes 2097152
Async XLA Ops:
  14.5 10.0 %copy-start.2 = (bf16[128,4096]{1,0:T(8,128)(2,1)S(1)}, bf16[128,4096]{1,0:T(8,128)(2,1)}, u32[]{:S(2)}) copy-start(bf16[128,4096]{1,0:T(8,128)(2,1)} %hid_ref.1) | copy-start | bytes 3145732
  14.5 10.0 %copy-start.3 = (s32[128]{0:T(128)S(1)}, s32[128]{0:T(128)}, u32[]{:S(2)}) copy-start(s32[128]{0:T(128)} %len_ref.1) | copy-start | bytes 1540
  24.5 39.1 %copy-start = (bf16[128,128,256]{2,1,0:T(8,128)(2,1)}, bf16[128,128,256]{2,1,0:T(8,128)(2,1)S(1)}, u32[]{:S(2)}) copy-start(bf16[128,128,256]{2,1,0:T(8,128)(2,1)S(1)} %get-tuple-element.18.vc_ref) | copy-start | bytes 25165828
  24.5 39.1 %copy-start.1 = (bf16[128,128,256]{2,1,0:T(8,128)(2,1)}, bf16[128,128,256]{2,1,0:T(8,128)(2,1)S(1)}, u32[]{:S(2)}) copy-start(bf16[128,128,256]{2,1,0:T(8,128)(2,1)S(1)} %get-tuple-element.17.kc_ref) | copy-start | bytes 25165828

commit v5 on v4

--- a/solution.py
+++ b/solution.py
@@ -48,10 +48,10 @@
     h_copy = pltpu.make_async_copy(hid_hbm, hid, sem_h)
     k_copy = pltpu.make_async_copy(wk_hbm.at[:, part], wkv.at[:, pl.ds(0, half)], sem_k)
     v_copy = pltpu.make_async_copy(wv_hbm.at[:, part], wkv.at[:, pl.ds(half, half)], sem_v)
-    for copy in (l_copy, n_copy, h_copy, k_copy, v_copy):
+    for copy in (h_copy, l_copy, n_copy, k_copy, v_copy):
         copy.start()
-    ahead = 3
-    for j in range(ahead):
+    ahead = 5
+    for j in range(2):
         q_copy(j).start()
     barrier = pltpu.get_barrier_semaphore()
     pl.semaphore_signal(barrier, inc=1, device_id=partner, device_id_type=MESH)
@@ -61,14 +61,16 @@
     across = lax.broadcasted_iota(jnp.int32, (rows, rows), 1)
     down = lax.broadcasted_iota(jnp.int32, (rows, rows), 0)
     column = jnp.sum(jnp.where(across == down, lengths, 0).astype(f32), axis=1, keepdims=True)
-    first = (me * slots).astype(f32)
-    slot_ref[...] = jnp.broadcast_to((column - first).astype(jnp.int32), slot_ref.shape)
+    slot = lax.broadcasted_iota(jnp.int32, (rows, slots), 1) + me * slots
+    slot_ref[...] = (slot.astype(f32) == column).astype(jnp.int32)
     angles = column * fr_ref[...]
     cos_t, sin_t = jnp.cos(angles), jnp.sin(angles)
 
     n_copy.wait()
     gain = 1.0 + wn[...].astype(f32).reshape(1, wn.shape[0])
     h_copy.wait()
+    for j in range(2, ahead):
+        q_copy(j).start()
     x = hid[...].astype(f32)
     inv_rms = lax.rsqrt(jnp.mean(x * x, axis=-1, keepdims=True) + EPSILON)
     xn[...] = (x * inv_rms * gain).astype(bf16)
@@ -250,10 +252,12 @@
     def l2(ph, half):
         return ring(ph, 4 + half, piece(ph, 2, half), from_right.at[ph, half], left)
 
-    def reduce_start(ph):
+    def reduce_far(ph):
         combine(ph, 0)
         r1(ph).start()
         l1(ph).start()
+
+    def reduce_near(ph):
         combine(ph, 1)
         r2(ph, 1).start()
         combine(ph, 2)
@@ -303,25 +307,21 @@
         part = pl.ds(u * per, per)
         return remote(gath.at[ph, c, part], other.at[ph, c, part], h_s.at[ph, which, u], h_r.at[ph, which, u], partner)
 
-    def project(ph, first):
+    def gather_rows(ph):
         at_copy(ph).wait_recv()
         for h in range(heads):
             for d in range(2):
                 pair = [att[ph, kk, d, pl.ds(h, CROWS, stride=heads), :] for kk in range(2)]
                 a_bf[ph, :, h * hd + d * hl:h * hd + (d + 1) * hl] = jnp.concatenate(pair, axis=0).astype(bf16)
 
-        def message(u, carry):
-            for v in range(per):
-                n = u * per + v
-                if first:
-                    wo_copy(n).wait()
-                y = jnp.dot(a_bf[ph], wo[n], preferred_element_type=f32)
-                gath[ph, chip, n] = hid_ref[rows_of(chip, ph), columns_of(core, n)].astype(f32) + y
-            for copy in own_copies(ph, u):
-                copy.start()
-            return carry
-
-        lax.fori_loop(0, nm, message, 0)
+    def project(ph, u):
+        for n in range(u * per, (u + 1) * per):
+            if ph == 0:
+                wo_copy(n).wait()
+            y = jnp.dot(a_bf[ph], wo[n], preferred_element_type=f32)
+            gath[ph, chip, n] = hid_ref[rows_of(chip, ph), columns_of(core, n)].astype(f32) + y
+        for copy in own_copies(ph, u):
+            copy.start()
 
     cl, cr, co = place_of(2), place_of(1), place_of(0)
     split = nm // 2
@@ -339,16 +339,15 @@
         for n in range(u * per, (u + 1) * per):
             out_ref[rows_of(c, ph), columns_of(mate, n)] = other[ph, c, n].astype(bf16)
 
-    def relay(ph):
-        for u in range(nm):
-            own_copies(ph, u)[0].wait_recv()
-            if u < split:
-                forward(ph, u).start()
-            to_mate(ph, 1, cl, u).start()
-            own_copies(ph, u)[1].wait_recv()
-            if u >= split:
-                forward(ph, u).start()
-            to_mate(ph, 2, cr, u).start()
+    def relay(ph, u):
+        own_copies(ph, u)[0].wait_recv()
+        if u < split:
+            forward(ph, u).start()
+        to_mate(ph, 1, cl, u).start()
+        own_copies(ph, u)[1].wait_recv()
+        if u >= split:
+            forward(ph, u).start()
+        to_mate(ph, 2, cr, u).start()
 
     def relay_end(ph):
         for u in range(nm):
@@ -383,20 +382,31 @@
     pl.semaphore_wait(barrier, 3)
     values_of(0)
     scores_of(1)
-    reduce_start(0)
+    reduce_far(0)
+    reduce_near(0)
     values_of(1)
+    reduce_far(1)
     reduce_turn(0)
-    reduce_start(1)
+    reduce_near(1)
     combine(0, 3)
+    combine(1, 3)
     reduce_turn(1)
-    combine(1, 3)
     reduce_end(0)
-    project(0, True)
+    gather_rows(0)
+    for u in range(split):
+        project(0, u)
     reduce_end(1)
-    project(1, False)
-    relay(0)
+    for u in range(split, nm):
+        project(0, u)
+    gather_rows(1)
+    for u in range(nm):
+        project(1, u)
+        relay(0, u)
+    for u in range(split):
+        relay(1, u)
     relay_end(0)
-    relay(1)
+    for u in range(split, nm):
+        relay(1, u)
     finish(0)
     relay_end(1)
     finish(1)
@@ -438,7 +448,7 @@
     q_all, k_rot, v_new, slot = pl.pallas_call(
         functools.partial(project_kernel, seq_block),
         out_shape=(pltpu.VMEM((2, nblk, 2, brows * hh, hl), f32), jax.ShapeDtypeStruct((rows, hd), bf16),
-                   jax.ShapeDtypeStruct((rows, hd), bf16), jax.ShapeDtypeStruct((rows, hd), jnp.int32)),
+                   jax.ShapeDtypeStruct((rows, hd), bf16), jax.ShapeDtypeStruct((rows, seq_block), jnp.int32)),
         in_specs=[hbm] * 3 + [vmem] + [hbm] * 3,
         out_specs=(vmem,) * 4,
         scratch_shapes=[
@@ -453,13 +463,13 @@
             pltpu.VMEM((hh, rows, hd), f32),
             dma, dma, dma, dma, dma, dma((hh,)), dma, dma, dma((hh,)), dma((hh,)),
         ],
-        compiler_params=pltpu.CompilerParams(collective_id=1, has_side_effects=True, vmem_limit_bytes=56 * MIB),
+        compiler_params=pltpu.CompilerParams(collective_id=1, has_side_effects=True, vmem_limit_bytes=48 * MIB),
         cost_estimate=pl.CostEstimate(flops=2 * rows * width * (hh + 1) * hd, bytes_accessed=2 * width * (hh + 1) * hd,
                                       transcendentals=0),
         name='project',
     )(keep(cache_len), keep(hidden), keep(w_norm), inv_freq, keep(w_k), keep(w_v), keep(w_q))
 
-    at_slot = lax.broadcasted_iota(jnp.int32, k_block.shape, 1) == slot[:, None, :]
+    at_slot = (slot != 0)[:, :, None]
     new_k_block = jnp.where(at_slot, k_rot[:, None, :], k_block)
     new_v_block = jnp.where(at_slot, v_new[:, None, :], v_block)
 

time: 64.7 us -> 54 us (0.83)
  Pallas kernels: 52.4 us -> 46.7 us
  other arithmetic: 10.5 us -> 5.45 us
    select_n x1, other arithmetic: 9.94 us -> 5.43 us  [local_step(): new_v_block = jnp.where(at_slot, v_new[:, None, :], v_block)]
    pallas_call x1, Pallas kernels: 39 us -> 35.6 us  [local_step(): pl.pallas_call(attend_kernel, out_shape=jax.ShapeDtypeStruct((rows, width...]
    pallas_call x1, Pallas kernels: 13.3 us -> 11.1 us  [local_step(): pl.pallas_call(functools.partial(project_kernel, seq_block), out_shape=(p...]
where the time goes in v5:
time: 54 us; the launch traced here: 53.9 us
  Pallas kernels  46.7 us (86%)
  other arithmetic  5.45 us (10%)
  local copies, waits for them, and re-layouts  1.01 us (2%)
  between operations  0.74 us (1%)
    pallas_call x1, Pallas kernels, local_step(): pl.pallas_call(attend_kernel, out_shape=jax.ShapeDtypeStruct((rows, width...  35.6 us
    pallas_call x1, Pallas kernels, local_step(): pl.pallas_call(functools.partial(project_kernel, seq_block), out_shape=(p...  11.1 us
    select_n x1, other arithmetic, local_step(): new_v_block = jnp.where(at_slot, v_new[:, None, :], v_block)  5.43 us

profile of v5, /device:TPU:81, one launch (start us, length us, event | category | flops | bytes accessed | tf_op | source)
XLA Modules:
  0.0 53.9 jit_solution(12687512977667641404)
XLA Ops:
  0.6 0.0 copy-start.4
  0.7 11.1 %project.1 = (f32[2,8,2,128,128]{4,3,2,1,0:T(8,128)S(1)}, bf16[128,256]{1,0:T(8,128)(2,1)S(1)}, bf16[128,256]{1,0:T(8,128)(2,1)S(1)}, s32[128,128]{1,0:T(8,128)S(1)}) custom-call(s32[128]{0:T(128)} %len_ref.1, bf16[128,4096]{1,0:T(8,128)(2,1)} %hid_ref.1, bf16[4096]{0:T(1024)(128)(2,1)} %wn_hbm.1, f32[1,128]{1,0:T(1,128)S(1)} %multiply_power_fusion.fr_ref, ...), custom_call_target="tpu_custom_call" | custom-call | flops 2415919104 | bytes 18874368 | tf_op jit(solution)/shard_map/project/pallas_call | solution.py:448
  11.8 0.0 copy-done.4
  11.8 0.0 copy-start.2
  11.8 0.0 copy-start.3
  11.8 5.4 %broadcast_select_fusion = (bf16[128,128,256]{2,1,0:T(8,128)(2,1)S(1)}, bf16[128,128,256]{2,1,0:T(8,128)(2,1)S(1)}) fusion(bf16[128,128,256]{2,1,0:T(8,128)(2,1)S(1)} %copy-done.4, pred[128,128]{1,0:T(8,128)(4,1)S(1)} %broadcast_compare_fusion, bf16[128,256]{1,0:T(8,128)(2,1)S(1)} %get-tuple-element.10, bf16[128,128,256]{2,1,0:T(8,128)(2,1)} %param.15, ...), kind=kLoop, calls=%fused_computation | loop fusion | flops 8388608 | bytes 33701888 | tf_op jit(solution)/shard_map/jit(_where)/select_n | solution.py:474
  17.2 0.0 copy-start
  17.3 0.0 copy-start.1
  17.3 0.0 copy-done.2
  17.3 0.0 copy-done.3
  17.3 35.6 %attend.1 = bf16[128,4096]{1,0:T(8,128)(2,1)S(1)} custom-call(s32[128]{0:T(128)S(1)} %copy-done.3, f32[2,8,2,128,128]{4,3,2,1,0:T(8,128)S(1)} %get-tuple-element.7.q_all, bf16[128,128,256]{2,1,0:T(8,128)(2,1)S(1)} %get-tuple-element.17.kc_ref, bf16[128,128,256]{2,1,0:T(8,128)(2,1)S(1)} %get-tuple-element.18.vc_ref, bf16[128,4096]{1,0:T(8,128)(2,1)S(1)} %copy-done.2, ...), custom_call_target="tpu_custom_call" | custom-call | flops 4294967296 | bytes 16777216 | tf_op jit(solution)/shard_map/attend/pallas_call | solution.py:478
  52.9 0.0 copy-done
  52.9 0.0 copy-done.1
  52.9 1.0 %copy.13 = bf16[128,4096]{1,0:T(8,128)(2,1)} copy(bf16[128,4096]{1,0:T(8,128)(2,1)S(1)} %attend.1) | data formatting | bytes 2097152
  (2 shorter events, 0.0 us)
Async XLA Ops:
  0.6 11.1 %copy-start.4 = (bf16[128,128,256]{2,1,0:T(8,128)(2,1)S(1)}, bf16[128,128,256]{2,1,0:T(8,128)(2,1)}, u32[]{:S(2)}) copy-start(bf16[128,128,256]{2,1,0:T(8,128)(2,1)} %param.16) | copy-start | bytes 25165828
  11.8 5.5 %copy-start.2 = (bf16[128,4096]{1,0:T(8,128)(2,1)S(1)}, bf16[128,4096]{1,0:T(8,128)(2,1)}, u32[]{:S(2)}) copy-start(bf16[128,4096]{1,0:T(8,128)(2,1)} %hid_ref.1) | copy-start | bytes 3145732
  11.8 5.5 %copy-start.3 = (s32[128]{0:T(128)S(1)}, s32[128]{0:T(128)}, u32[]{:S(2)}) copy-start(s32[128]{0:T(128)} %len_ref.1) | copy-start | bytes 1540
  17.2 35.6 %copy-start = (bf16[128,128,256]{2,1,0:T(8,128)(2,1)}, bf16[128,128,256]{2,1,0:T(8,128)(2,1)S(1)}, u32[]{:S(2)}) copy-start(bf16[128,128,256]{2,1,0:T(8,128)(2,1)S(1)} %get-tuple-element.18.vc_ref) | copy-start | bytes 25165828
  17.3 35.6 %copy-start.1 = (bf16[128,128,256]{2,1,0:T(8,128)(2,1)}, bf16[128,128,256]{2,1,0:T(8,128)(2,1)S(1)}, u32[]{:S(2)}) copy-start(bf16[128,128,256]{2,1,0:T(8,128)(2,1)S(1)} %get-tuple-element.17.kc_ref) | copy-start | bytes 25165828

commit v6 on v5

--- a/solution.py
+++ b/solution.py
@@ -363,34 +363,30 @@
                 to_mate(ph, which, c, u).wait_recv()
                 put_other(ph, c, u)
 
-    def scores_of(ph):
+    def units(ph, first, last, send):
         def body(t, carry):
             scores(ph, t)
+            values(ph, t)
+            if send:
+                d_copy(ph, t).start()
             return carry
 
-        lax.fori_loop(0, CHIPS, body, 0)
-
-    def values_of(ph):
-        def body(t, carry):
-            values(ph, t)
-            d_copy(ph, t).start()
-            return carry
-
-        lax.fori_loop(0, CHIPS, body, 0)
-
-    scores_of(0)
+        lax.fori_loop(first, last, body, 0)
+
+    units(0, 0, 2, False)
     pl.semaphore_wait(barrier, 3)
-    values_of(0)
-    scores_of(1)
+    d_copy(0, 0).start()
+    d_copy(0, 1).start()
+    units(0, 2, CHIPS, True)
     reduce_far(0)
     reduce_near(0)
-    values_of(1)
+    units(1, 0, CHIPS, True)
     reduce_far(1)
     reduce_turn(0)
     reduce_near(1)
     combine(0, 3)
+    reduce_turn(1)
     combine(1, 3)
-    reduce_turn(1)
     reduce_end(0)
     gather_rows(0)
     for u in range(split):
@@ -398,10 +394,13 @@
     reduce_end(1)
     for u in range(split, nm):
         project(0, u)
+    for u in range(split):
+        relay(0, u)
     gather_rows(1)
     for u in range(nm):
         project(1, u)
-        relay(0, u)
+        if u < nm - split:
+            relay(0, split + u)
     for u in range(split):
         relay(1, u)
     relay_end(0)

time: 54 us -> 51.6 us (0.956)
  Pallas kernels: 46.7 us -> 44.3 us
    pallas_call x1, Pallas kernels: 35.6 us -> 33.2 us  [local_step(): pl.pallas_call(attend_kernel, out_shape=jax.ShapeDtypeStruct((rows, width...]
where the time goes in v6:
time: 51.6 us; the launch traced here: 51.5 us
  Pallas kernels  44.3 us (86%)
  other arithmetic  5.45 us (11%)
  local copies, waits for them, and re-layouts  1.01 us (2%)
  between operations  0.74 us (1%)
    pallas_call x1, Pallas kernels, local_step(): pl.pallas_call(attend_kernel, out_shape=jax.ShapeDtypeStruct((rows, width...  33.2 us
    pallas_call x1, Pallas kernels, local_step(): pl.pallas_call(functools.partial(project_kernel, seq_block), out_shape=(p...  11.1 us
    select_n x1, other arithmetic, local_step(): new_v_block = jnp.where(at_slot, v_new[:, None, :], v_block)  5.43 us

profile of v6, /device:TPU:81, one launch (start us, length us, event | category | flops | bytes accessed | tf_op | source)
XLA Modules:
  0.0 51.5 jit_solution(15165507538945940111)
XLA Ops:
  0.6 0.0 copy-start.4
  0.7 11.1 %project.1 = (f32[2,8,2,128,128]{4,3,2,1,0:T(8,128)S(1)}, bf16[128,256]{1,0:T(8,128)(2,1)S(1)}, bf16[128,256]{1,0:T(8,128)(2,1)S(1)}, s32[128,128]{1,0:T(8,128)S(1)}) custom-call(s32[128]{0:T(128)} %len_ref.1, bf16[128,4096]{1,0:T(8,128)(2,1)} %hid_ref.1, bf16[4096]{0:T(1024)(128)(2,1)} %wn_hbm.1, f32[1,128]{1,0:T(1,128)S(1)} %multiply_power_fusion.fr_ref, ...), custom_call_target="tpu_custom_call" | custom-call | flops 2415919104 | bytes 18874368 | tf_op jit(solution)/shard_map/project/pallas_call | solution.py:447
  11.8 0.0 copy-done.4
  11.8 0.0 copy-start.2
  11.8 0.0 copy-start.3
  11.8 5.4 %broadcast_select_fusion = (bf16[128,128,256]{2,1,0:T(8,128)(2,1)S(1)}, bf16[128,128,256]{2,1,0:T(8,128)(2,1)S(1)}) fusion(bf16[128,128,256]{2,1,0:T(8,128)(2,1)S(1)} %copy-done.4, pred[128,128]{1,0:T(8,128)(4,1)S(1)} %broadcast_compare_fusion, bf16[128,256]{1,0:T(8,128)(2,1)S(1)} %get-tuple-element.10, bf16[128,128,256]{2,1,0:T(8,128)(2,1)} %param.15, ...), kind=kLoop, calls=%fused_computation | loop fusion | flops 8388608 | bytes 33701888 | tf_op jit(solution)/shard_map/jit(_where)/select_n | solution.py:473
  17.2 0.0 copy-start
  17.3 0.0 copy-start.1
  17.3 0.0 copy-done.2
  17.3 0.0 copy-done.3
  17.3 33.2 %attend.1 = bf16[128,4096]{1,0:T(8,128)(2,1)S(1)} custom-call(s32[128]{0:T(128)S(1)} %copy-done.3, f32[2,8,2,128,128]{4,3,2,1,0:T(8,128)S(1)} %get-tuple-element.7.q_all, bf16[128,128,256]{2,1,0:T(8,128)(2,1)S(1)} %get-tuple-element.17.kc_ref, bf16[128,128,256]{2,1,0:T(8,128)(2,1)S(1)} %get-tuple-element.18.vc_ref, bf16[128,4096]{1,0:T(8,128)(2,1)S(1)} %copy-done.2, ...), custom_call_target="tpu_custom_call" | custom-call | flops 4294967296 | bytes 16777216 | tf_op jit(solution)/shard_map/attend/pallas_call | solution.py:477
  50.5 0.0 copy-done
  50.5 0.0 copy-done.1
  50.5 1.0 %copy.13 = bf16[128,4096]{1,0:T(8,128)(2,1)} copy(bf16[128,4096]{1,0:T(8,128)(2,1)S(1)} %attend.1) | data formatting | bytes 2097152
  (2 shorter events, 0.0 us)
Async XLA Ops:
  0.6 11.1 %copy-start.4 = (bf16[128,128,256]{2,1,0:T(8,128)(2,1)S(1)}, bf16[128,128,256]{2,1,0:T(8,128)(2,1)}, u32[]{:S(2)}) copy-start(bf16[128,128,256]{2,1,0:T(8,128)(2,1)} %param.16) | copy-start | bytes 25165828
  11.8 5.5 %copy-start.2 = (bf16[128,4096]{1,0:T(8,128)(2,1)S(1)}, bf16[128,4096]{1,0:T(8,128)(2,1)}, u32[]{:S(2)}) copy-start(bf16[128,4096]{1,0:T(8,128)(2,1)} %hid_ref.1) | copy-start | bytes 3145732
  11.8 5.5 %copy-start.3 = (s32[128]{0:T(128)S(1)}, s32[128]{0:T(128)}, u32[]{:S(2)}) copy-start(s32[128]{0:T(128)} %len_ref.1) | copy-start | bytes 1540
  17.2 33.2 %copy-start = (bf16[128,128,256]{2,1,0:T(8,128)(2,1)}, bf16[128,128,256]{2,1,0:T(8,128)(2,1)S(1)}, u32[]{:S(2)}) copy-start(bf16[128,128,256]{2,1,0:T(8,128)(2,1)S(1)} %get-tuple-element.18.vc_ref) | copy-start | bytes 25165828
  17.3 33.2 %copy-start.1 = (bf16[128,128,256]{2,1,0:T(8,128)(2,1)}, bf16[128,128,256]{2,1,0:T(8,128)(2,1)S(1)}, u32[]{:S(2)}) copy-start(bf16[128,128,256]{2,1,0:T(8,128)(2,1)S(1)} %get-tuple-element.17.kc_ref) | copy-start | bytes 25165828

commit v7 on v6

--- a/solution.py
+++ b/solution.py
@@ -22,7 +22,7 @@
     return jnp.concatenate([low * cos_t - high * sin_t, high * cos_t + low * sin_t], axis=-1)
 
 
-def project_kernel(slots, len_hbm, hid_hbm, wn_hbm, fr_ref, wk_hbm, wv_hbm, wq_hbm, q_ref, k_ref, v_ref, slot_ref,
+def project_kernel(slots, len_hbm, hid_hbm, wn_hbm, fr_ref, wk_hbm, wv_hbm, wq_hbm, q_ref, k_ref, v_ref, slot_ref, last_ref,
                    lens, wn, hid, xn, wkv, wq, kv, mine, theirs, sem_l, sem_n, sem_h, sem_k, sem_v, sem_q, kv_s, kv_r,
                    x_s, x_r):
     f32, bf16 = jnp.float32, jnp.bfloat16
@@ -63,6 +63,7 @@
     column = jnp.sum(jnp.where(across == down, lengths, 0).astype(f32), axis=1, keepdims=True)
     slot = lax.broadcasted_iota(jnp.int32, (rows, slots), 1) + me * slots
     slot_ref[...] = (slot.astype(f32) == column).astype(jnp.int32)
+    last_ref[...] = jnp.broadcast_to(column.astype(jnp.int32) - me * slots, last_ref.shape)
     angles = column * fr_ref[...]
     cos_t, sin_t = jnp.cos(angles), jnp.sin(angles)
 
@@ -127,7 +128,7 @@
     lax.fori_loop(0, heads, finish, 0)
 
 
-def attend_kernel(len_ref, q_all, kc_ref, vc_ref, hid_ref, wo_hbm, out_ref,
+def attend_kernel(last_ref, q_all, kc_ref, vc_ref, hid_ref, wo_hbm, out_ref,
                   p_buf, mine, theirs, r_recv, l_recv, from_left, from_right, att, a_bf, wo, gath, other,
                   sem_wo, d_s, d_r, rs_s, rs_r, at_s, at_r, own_s, own_r, fw_s, fw_r, h_s, h_r):
     f32, bf16 = jnp.float32, jnp.bfloat16
@@ -171,7 +172,6 @@
     lane = lax.broadcasted_iota(jnp.int32, (heads, slots), 1)
     lane8 = lax.broadcasted_iota(jnp.int32, (8, 128), 1)
     is_max = lane8 < 64
-    position = me * slots + lane
 
     def place_of(t):
         return lax.rem(chip + 2 - t + 3 * (t // 2) - 2 * (t // 3), CHIPS)
@@ -188,7 +188,7 @@
                     q = jnp.concatenate([
                         jnp.concatenate([q_all[k, i, d, own_rows, :] for k in range(2)], axis=0) for d in range(2)], axis=1)
                     s = lax.dot_general(q.astype(bf16), kc_ref[b], (((1,), (1,)), ((), ())), preferred_element_type=f32)
-                    valid = position <= len_ref[b]
+                    valid = lane <= last_ref[pl.ds(b, 1), :]
                     s = jnp.where(valid, s, LOWEST)
                     m = jnp.max(s, axis=1, keepdims=True)
                     p = jnp.where(valid, jnp.exp(s - m), 0.0)
@@ -326,10 +326,10 @@
     cl, cr, co = place_of(2), place_of(1), place_of(0)
     split = nm // 2
 
-    def forward(ph, u):
-        c, dev = (cl, right) if u < split else (cr, left)
-        src = gath.at[ph, c, pl.ds(u * per, per)]
-        return remote(src, src, fw_s.at[ph, u], fw_r.at[ph, u], dev)
+    def forward(ph, way, u):
+        c, dev = (cl, right) if way == 0 else (cr, left)
+        src = gath.at[ph, c, pl.ds(u * per + way * (per // 2), per // 2)]
+        return remote(src, src, fw_s.at[ph, way, u], fw_r.at[ph, way, u], dev)
 
     def put(ph, c, u):
         for n in range(u * per, (u + 1) * per):
@@ -341,17 +341,16 @@
 
     def relay(ph, u):
         own_copies(ph, u)[0].wait_recv()
-        if u < split:
-            forward(ph, u).start()
+        forward(ph, 0, u).start()
         to_mate(ph, 1, cl, u).start()
         own_copies(ph, u)[1].wait_recv()
-        if u >= split:
-            forward(ph, u).start()
+        forward(ph, 1, u).start()
         to_mate(ph, 2, cr, u).start()
 
     def relay_end(ph):
         for u in range(nm):
-            forward(ph, u).wait_recv()
+            for way in range(2):
+                forward(ph, way, u).wait_recv()
             to_mate(ph, 3, co, u).start()
 
     places = ((0, chip), (1, cl), (2, cr), (3, co))
@@ -418,7 +417,8 @@
         for u in range(nm):
             for copy in own_copies(ph, u):
                 copy.wait_send()
-            forward(ph, u).wait_send()
+            for way in range(2):
+                forward(ph, way, u).wait_send()
             for which, c in places[1:]:
                 to_mate(ph, which, c, u).wait_send()
 
@@ -435,7 +435,6 @@
     inv_freq = (ROPE_BASE ** (-jnp.arange(hl, dtype=f32) * 2.0 / hd)).reshape(1, hl)
     vmem = pl.BlockSpec(memory_space=pltpu.VMEM)
     hbm = pl.BlockSpec(memory_space=pl.ANY)
-    smem = pl.BlockSpec(memory_space=pltpu.SMEM)
     dma = pltpu.SemaphoreType.DMA
 
     def keep(x):
@@ -444,12 +443,13 @@
     def near(x):
         return pltpu.with_memory_space_constraint(x, pltpu.VMEM)
 
-    q_all, k_rot, v_new, slot = pl.pallas_call(
+    q_all, k_rot, v_new, slot, last = pl.pallas_call(
         functools.partial(project_kernel, seq_block),
         out_shape=(pltpu.VMEM((2, nblk, 2, brows * hh, hl), f32), jax.ShapeDtypeStruct((rows, hd), bf16),
-                   jax.ShapeDtypeStruct((rows, hd), bf16), jax.ShapeDtypeStruct((rows, seq_block), jnp.int32)),
+                   jax.ShapeDtypeStruct((rows, hd), bf16), jax.ShapeDtypeStruct((rows, seq_block), jnp.int32),
+                   jax.ShapeDtypeStruct((rows, seq_block), jnp.int32)),
         in_specs=[hbm] * 3 + [vmem] + [hbm] * 3,
-        out_specs=(vmem,) * 4,
+        out_specs=(vmem,) * 5,
         scratch_shapes=[
             pltpu.VMEM((rows,), jnp.int32),
             pltpu.VMEM((width,), bf16),
@@ -477,7 +477,7 @@
     out_hidden = pl.pallas_call(
         attend_kernel,
         out_shape=jax.ShapeDtypeStruct((rows, width), bf16),
-        in_specs=[smem, vmem, vmem, vmem, vmem, hbm],
+        in_specs=[vmem, vmem, vmem, vmem, vmem, hbm],
         out_specs=vmem,
         scratch_shapes=[
             pltpu.VMEM((CHIPS, brows, heads, seq_block), bf16),
@@ -493,13 +493,13 @@
             pltpu.VMEM((2, CHIPS, hh, brows, hd), f32),
             pltpu.VMEM((2, CHIPS, hh, brows, hd), f32),
             dma((hh,)), dma((2, CHIPS)), dma((2, CHIPS)), dma((2, 6)), dma((2, 6)), dma((2,)), dma((2,)),
-            dma((2, 2, nm)), dma((2, 2, nm)), dma((2, nm)), dma((2, nm)), dma((2, CHIPS, nm)), dma((2, CHIPS, nm)),
+            dma((2, 2, nm)), dma((2, 2, nm)), dma((2, 2, nm)), dma((2, 2, nm)), dma((2, CHIPS, nm)), dma((2, CHIPS, nm)),
         ],
         compiler_params=pltpu.CompilerParams(collective_id=0, has_side_effects=True, vmem_limit_bytes=26 * MIB),
         cost_estimate=pl.CostEstimate(flops=2 * rows * width * hh * hd * 2, bytes_accessed=2 * width * hh * hd,
                                       transcendentals=0),
         name='attend',
-    )(cache_len, near(q_all), near(new_k_block), near(new_v_block), hidden, keep(w_o))
+    )(last, near(q_all), near(new_k_block), near(new_v_block), hidden, keep(w_o))
     return out_hidden, new_k_block, new_v_block
 
 

time: 51.6 us -> 51.3 us (level)
  no operation moved by 1% of the time
where the time goes in v7:
time: 51.3 us; the launch traced here: 51.2 us
  Pallas kernels  44.1 us (86%)
  other arithmetic  5.38 us (10%)
  local copies, waits for them, and re-layouts  1 us (2%)
  between operations  0.73 us (1%)
    pallas_call x1, Pallas kernels, local_step(): pl.pallas_call(attend_kernel, out_shape=jax.ShapeDtypeStruct((rows, width...  33 us
    pallas_call x1, Pallas kernels, local_step(): pl.pallas_call(functools.partial(project_kernel, seq_block), out_shape=(p...  11.1 us
    select_n x1, other arithmetic, local_step(): new_v_block = jnp.where(at_slot, v_new[:, None, :], v_block)  5.36 us

profile of v7, /device:TPU:81, one launch (start us, length us, event | category | flops | bytes accessed | tf_op | source)
XLA Modules:
  0.0 51.2 jit_solution(13306553393788446266)
XLA Ops:
  0.6 0.0 copy-start.3
  0.7 11.1 %project.1 = (f32[2,8,2,128,128]{4,3,2,1,0:T(8,128)S(1)}, bf16[128,256]{1,0:T(8,128)(2,1)S(1)}, bf16[128,256]{1,0:T(8,128)(2,1)S(1)}, s32[128,128]{1,0:T(8,128)S(1)}, s32[128,128]{1,0:T(8,128)S(1)}) custom-call(s32[128]{0:T(128)} %len_hbm.1, bf16[128,4096]{1,0:T(8,128)(2,1)} %hid_ref.1, bf16[4096]{0:T(1024)(128)(2,1)} %wn_hbm.1, ...), custom_call_target="tpu_custom_call" | custom-call | flops 2415919104 | bytes 18874368 | tf_op jit(solution)/shard_map/project/pallas_call | solution.py:446
  11.8 0.0 copy-done.3
  11.8 0.0 copy-start.2
  11.8 5.4 %broadcast_select_fusion = (bf16[128,128,256]{2,1,0:T(8,128)(2,1)S(1)}, bf16[128,128,256]{2,1,0:T(8,128)(2,1)S(1)}) fusion(bf16[128,128,256]{2,1,0:T(8,128)(2,1)S(1)} %copy-done.3, pred[128,128]{1,0:T(8,128)(4,1)S(1)} %broadcast_compare_fusion, bf16[128,256]{1,0:T(8,128)(2,1)S(1)} %get-tuple-element.12, bf16[128,128,256]{2,1,0:T(8,128)(2,1)} %param.15, ...), kind=kLoop, calls=%fused_computation | loop fusion | flops 8388608 | bytes 33701888 | tf_op jit(solution)/shard_map/jit(_where)/select_n | solution.py:473
  17.2 0.0 copy-start
  17.2 0.0 copy-start.1
  17.2 0.0 copy-done.2
  17.2 33.0 %attend.1 = bf16[128,4096]{1,0:T(8,128)(2,1)S(1)} custom-call(s32[128,128]{1,0:T(8,128)S(1)} %get-tuple-element.8.last_ref, f32[2,8,2,128,128]{4,3,2,1,0:T(8,128)S(1)} %get-tuple-element.9.q_all, bf16[128,128,256]{2,1,0:T(8,128)(2,1)S(1)} %get-tuple-element.19.kc_ref, bf16[128,128,256]{2,1,0:T(8,128)(2,1)S(1)} %get-tuple-element.20.vc_ref, ...), custom_call_target="tpu_custom_call" | custom-call | flops 4294967296 | bytes 16777216 | tf_op jit(solution)/shard_map/attend/pallas_call | solution.py:477
  50.2 0.0 copy-done
  50.2 0.0 copy-done.1
  50.2 1.0 %copy.13 = bf16[128,4096]{1,0:T(8,128)(2,1)} copy(bf16[128,4096]{1,0:T(8,128)(2,1)S(1)} %attend.1) | data formatting | bytes 2097152
  (2 shorter events, 0.0 us)
Async XLA Ops:
  0.6 11.1 %copy-start.3 = (bf16[128,128,256]{2,1,0:T(8,128)(2,1)S(1)}, bf16[128,128,256]{2,1,0:T(8,128)(2,1)}, u32[]{:S(2)}) copy-start(bf16[128,128,256]{2,1,0:T(8,128)(2,1)} %param.16) | copy-start | bytes 25165828
  11.8 5.4 %copy-start.2 = (bf16[128,4096]{1,0:T(8,128)(2,1)S(1)}, bf16[128,4096]{1,0:T(8,128)(2,1)}, u32[]{:S(2)}) copy-start(bf16[128,4096]{1,0:T(8,128)(2,1)} %hid_ref.1) | copy-start | bytes 3145732
  17.2 33.1 %copy-start = (bf16[128,128,256]{2,1,0:T(8,128)(2,1)}, bf16[128,128,256]{2,1,0:T(8,128)(2,1)S(1)}, u32[]{:S(2)}) copy-start(bf16[128,128,256]{2,1,0:T(8,128)(2,1)S(1)} %get-tuple-element.20.vc_ref) | copy-start | bytes 25165828
  17.2 33.0 %copy-start.1 = (bf16[128,128,256]{2,1,0:T(8,128)(2,1)}, bf16[128,128,256]{2,1,0:T(8,128)(2,1)S(1)}, u32[]{:S(2)}) copy-start(bf16[128,128,256]{2,1,0:T(8,128)(2,1)S(1)} %get-tuple-element.19.kc_ref) | copy-start | bytes 25165828

commit v8 on v7

--- a/solution.py
+++ b/solution.py
@@ -352,15 +352,17 @@
             for way in range(2):
                 forward(ph, way, u).wait_recv()
             to_mate(ph, 3, co, u).start()
+            put(ph, co, u)
 
     places = ((0, chip), (1, cl), (2, cr), (3, co))
 
-    def finish(ph):
-        for which, c in places:
-            for u in range(nm):
+    def finish(ph, which):
+        c = places[which][1]
+        for u in range(nm):
+            if which < 3:
                 put(ph, c, u)
-                to_mate(ph, which, c, u).wait_recv()
-                put_other(ph, c, u)
+            to_mate(ph, which, c, u).wait_recv()
+            put_other(ph, c, u)
 
     def units(ph, first, last, send):
         def body(t, carry):
@@ -381,9 +383,9 @@
     reduce_near(0)
     units(1, 0, CHIPS, True)
     reduce_far(1)
+    combine(0, 3)
     reduce_turn(0)
     reduce_near(1)
-    combine(0, 3)
     reduce_turn(1)
     combine(1, 3)
     reduce_end(0)
@@ -405,9 +407,12 @@
     relay_end(0)
     for u in range(split, nm):
         relay(1, u)
-    finish(0)
+    for which in range(4):
+        finish(0, which)
+    for which in range(3):
+        finish(1, which)
     relay_end(1)
-    finish(1)
+    finish(1, 3)
 
     for ph in range(2):
         for t in range(CHIPS):

time: 51.3 us -> 51.3 us (level)
  no operation moved by 1% of the time
where the time goes in v8:
time: 51.3 us; the launch traced here: 51.2 us
  Pallas kernels  44.1 us (86%)
  other arithmetic  5.38 us (10%)
  local copies, waits for them, and re-layouts  1 us (2%)
  between operations  0.73 us (1%)
    pallas_call x1, Pallas kernels, local_step(): pl.pallas_call(attend_kernel, out_shape=jax.ShapeDtypeStruct((rows, width...  33 us
    pallas_call x1, Pallas kernels, local_step(): pl.pallas_call(functools.partial(project_kernel, seq_block), out_shape=(p...  11.1 us
    select_n x1, other arithmetic, local_step(): new_v_block = jnp.where(at_slot, v_new[:, None, :], v_block)  5.36 us

profile of v8, /device:TPU:81, one launch (start us, length us, event | category | flops | bytes accessed | tf_op | source)
XLA Modules:
  0.0 51.2 jit_solution(16024584785296166029)
XLA Ops:
  0.6 0.0 copy-start.3
  0.7 11.1 %project.1 = (f32[2,8,2,128,128]{4,3,2,1,0:T(8,128)S(1)}, bf16[128,256]{1,0:T(8,128)(2,1)S(1)}, bf16[128,256]{1,0:T(8,128)(2,1)S(1)}, s32[128,128]{1,0:T(8,128)S(1)}, s32[128,128]{1,0:T(8,128)S(1)}) custom-call(s32[128]{0:T(128)} %len_hbm.1, bf16[128,4096]{1,0:T(8,128)(2,1)} %hid_ref.1, bf16[4096]{0:T(1024)(128)(2,1)} %wn_hbm.1, ...), custom_call_target="tpu_custom_call" | custom-call | flops 2415919104 | bytes 18874368 | tf_op jit(solution)/shard_map/project/pallas_call | solution.py:451
  11.8 0.0 copy-done.3
  11.8 0.0 copy-start.2
  11.8 5.4 %broadcast_select_fusion = (bf16[128,128,256]{2,1,0:T(8,128)(2,1)S(1)}, bf16[128,128,256]{2,1,0:T(8,128)(2,1)S(1)}) fusion(bf16[128,128,256]{2,1,0:T(8,128)(2,1)S(1)} %copy-done.3, pred[128,128]{1,0:T(8,128)(4,1)S(1)} %broadcast_compare_fusion, bf16[128,256]{1,0:T(8,128)(2,1)S(1)} %get-tuple-element.12, bf16[128,128,256]{2,1,0:T(8,128)(2,1)} %param.15, ...), kind=kLoop, calls=%fused_computation | loop fusion | flops 8388608 | bytes 33701888 | tf_op jit(solution)/shard_map/jit(_where)/select_n | solution.py:478
  17.2 0.0 copy-start
  17.2 0.0 copy-start.1
  17.2 0.0 copy-done.2
  17.2 33.0 %attend.1 = bf16[128,4096]{1,0:T(8,128)(2,1)S(1)} custom-call(s32[128,128]{1,0:T(8,128)S(1)} %get-tuple-element.8.last_ref, f32[2,8,2,128,128]{4,3,2,1,0:T(8,128)S(1)} %get-tuple-element.9.q_all, bf16[128,128,256]{2,1,0:T(8,128)(2,1)S(1)} %get-tuple-element.19.kc_ref, bf16[128,128,256]{2,1,0:T(8,128)(2,1)S(1)} %get-tuple-element.20.vc_ref, ...), custom_call_target="tpu_custom_call" | custom-call | flops 4294967296 | bytes 16777216 | tf_op jit(solution)/shard_map/attend/pallas_call | solution.py:482
  50.2 0.0 copy-done
  50.2 0.0 copy-done.1
  50.2 1.0 %copy.13 = bf16[128,4096]{1,0:T(8,128)(2,1)} copy(bf16[128,4096]{1,0:T(8,128)(2,1)S(1)} %attend.1) | data formatting | bytes 2097152
  (2 shorter events, 0.0 us)
Async XLA Ops:
  0.6 11.1 %copy-start.3 = (bf16[128,128,256]{2,1,0:T(8,128)(2,1)S(1)}, bf16[128,128,256]{2,1,0:T(8,128)(2,1)}, u32[]{:S(2)}) copy-start(bf16[128,128,256]{2,1,0:T(8,128)(2,1)} %param.16) | copy-start | bytes 25165828
  11.8 5.4 %copy-start.2 = (bf16[128,4096]{1,0:T(8,128)(2,1)S(1)}, bf16[128,4096]{1,0:T(8,128)(2,1)}, u32[]{:S(2)}) copy-start(bf16[128,4096]{1,0:T(8,128)(2,1)} %hid_ref.1) | copy-start | bytes 3145732
  17.2 33.1 %copy-start = (bf16[128,128,256]{2,1,0:T(8,128)(2,1)}, bf16[128,128,256]{2,1,0:T(8,128)(2,1)S(1)}, u32[]{:S(2)}) copy-start(bf16[128,128,256]{2,1,0:T(8,128)(2,1)S(1)} %get-tuple-element.20.vc_ref) | copy-start | bytes 25165828
  17.2 33.0 %copy-start.1 = (bf16[128,128,256]{2,1,0:T(8,128)(2,1)}, bf16[128,128,256]{2,1,0:T(8,128)(2,1)S(1)}, u32[]{:S(2)}) copy-start(bf16[128,128,256]{2,1,0:T(8,128)(2,1)S(1)} %get-tuple-element.19.kc_ref) | copy-start | bytes 25165828
